TPU v7x, 512 devices: a whole 4x4x16 slice. The times are simulated.
512 devices in a mesh: dp: 32 (over y_hi, z), mp: 16 (over x, y_lo, core).
Axes of the slice: x: 4, y: 4 (y_hi: 2, y_lo: 2; y = y_hi * 2 + y_lo), z: 16, core: 2. Of those that a mesh axis runs over, the one named last changes fastest.
Arguments:
- tokens: bfloat16 [32768, 4096], P('dp', 'mp'), may hold values from -6 to 6
- right_weight: bfloat16 [64, 64, 64], P('mp', 'dp'), may hold values from -0.75 to 0.75
- left_weight: bfloat16 [64, 64, 64], P('mp', 'dp'), may hold values from -0.75 to 0.75
- cotangent: bfloat16 [32768, 4096], P('dp', 'mp'), may hold values from -0.032958984 to 0.032958984
Outputs:
- activated: bfloat16 [32768, 4096], P('dp', 'mp')
- grad_right: float32 [64, 64, 64], P('mp', 'dp')
- grad_left: float32 [64, 64, 64], P('mp', 'dp')
All inputs are finite; a program needn't handle non-finite values.
Results may differ from a plain program's by a relative error of at most 0.0056.
Values may be sent and summed in bfloat16 or wider, within the bound.
No kernel may reach another device: no remote copies, remote signals or barrier semaphores. Data moves between devices by JAX's collectives and lax.ppermute only.
A program may use at most 64 MiB of HBM per device.

v0:
```python
import jax
import jax.numpy as jnp
from jax import lax
from jax.sharding import PartitionSpec as P

NB = 64
BS = 64


def in_order(parts, dim):
    dims = list(parts.shape[1:])
    dims[dim] *= parts.shape[0]
    return jnp.moveaxis(parts, 0, dim).reshape(dims)


def gather_together(arrays, axis, dims):
    line = jnp.concatenate([a.reshape(-1) for a in arrays])
    lines, at, gathered = (lax.all_gather(line, axis), 0, [])
    for a, dim in zip(arrays, dims):
        parts = lines[:, at : at + a.size].reshape(-1, *a.shape)
        gathered.append(in_order(parts, dim))
        at += a.size
    return tuple(gathered)


def cut_along(x, dim, devices):
    before, after = (x.shape[:dim], x.shape[dim + 1 :])
    return jnp.moveaxis(x.reshape(*before, devices, -1, *after), dim, 0)


def sent_and_summed(x, axis, dim):
    devices = lax.axis_size(axis)
    parts = lax.all_to_all(cut_along(x, dim, devices), axis, 0, 0, tiled=True)
    return jnp.sum(parts, axis=0)


def in_one_piece(arrays, axis, dim, along):
    widths = [a.shape[along] for a in arrays]
    both = jnp.concatenate(arrays, axis=along)
    result = sent_and_summed(both, axis, dim)
    return tuple(jnp.split(result, [sum(widths[:k]) for k in range(1, len(widths))], axis=along))


def gelu_slope(pre):
    cdf = 0.5 * (1.0 + lax.erf(pre * 0.7071067811865476))
    density = jnp.exp(-0.5 * pre * pre) * 0.3989422804014327
    return cdf + pre * density


def shards(tokens, right_weight, left_weight, cotangent):
    tok_rows = tokens.shape[0]
    groups = lax.axis_size("mp")
    owned = NB // groups
    right_rows, left_rows = gather_together((right_weight, left_weight), "dp", (1, 1))
    xs = tokens.reshape(tok_rows, owned, BS)
    inner = jnp.einsum("tik,ikm->tmi", xs, right_rows, preferred_element_type=jnp.float32)
    inner = inner.astype(jnp.bfloat16).reshape(tok_rows, BS * owned)
    left_four = left_rows.reshape(owned, groups, owned, BS)
    received = lax.all_to_all(inner, "mp", split_axis=1, concat_axis=1, tiled=True)
    rows = received.shape[0]
    mixed = received.reshape(rows, groups, owned, owned)
    pre_rows = jnp.einsum("tpmj,mpjn->tmn", mixed, left_four, preferred_element_type=jnp.float32)
    received, pre = (received, pre_rows)
    mixed = received.reshape(tok_rows, groups, owned, owned)
    activated = (
        jax.nn.gelu(pre, approximate=False).astype(jnp.bfloat16).reshape(tok_rows, owned * BS)
    )
    dpre = (cotangent.reshape(tok_rows, owned, BS).astype(jnp.float32) * gelu_slope(pre)).astype(
        jnp.bfloat16
    )
    part_left = jnp.einsum("tpmj,tmn->mpjn", mixed, dpre, preferred_element_type=jnp.float32)
    part_left = part_left.reshape(owned, NB, BS)
    dmixed = jnp.einsum("tmn,mpjn->tpmj", dpre, left_four, preferred_element_type=jnp.float32)
    dmixed = dmixed.astype(jnp.bfloat16).reshape(tok_rows, groups * owned * owned)
    dinner = lax.all_to_all(dmixed, "mp", split_axis=1, concat_axis=1, tiled=True)
    dinner = dinner.reshape(tok_rows, groups, owned, owned)
    part_right = jnp.einsum("tik,tqmi->ikqm", xs, dinner, preferred_element_type=jnp.float32)
    part_right = part_right.reshape(owned, BS, BS)
    grad_right, grad_left = in_one_piece((part_right, part_left), "dp", 1, 0)
    return (activated, grad_right, grad_left)


def solution(mesh):
    return jax.shard_map(
        shards,
        mesh=mesh,
        in_specs=(P("dp", "mp"), P("mp", "dp", None), P("mp", "dp", None), P("dp", "mp")),
        out_specs=(P("dp", "mp"), P("mp", "dp", None), P("mp", "dp", None)),
        check_vma=False,
    )
```

profile of v0, /device:TPU:1, one launch (start us, length us, event | category | flops | bytes accessed | tf_op | source)
XLA Modules:
  0.0 150.1 jit_solution(9016281412636657445)
XLA Ops:
  0.6 0.8 reshape.55
  1.4 0.8 reshape.54
  2.2 69.5 %all-gather = bf16[32768]{0:T(1024)(128)(2,1)S(1)} all-gather(bf16[1024]{0:T(1024)(128)(2,1)S(1)} %pad_maximum_fusion), channel_id=2, replica_groups=mesh['dp'=32,'mp'=16] {'dp'}, dimensions={0}, use_global_device_ids=true | all-gather | bytes 67584 | tf_op jit(solution)/shard_map/all_gather | solution.py:18
  71.7 0.1 reshape.57
  71.8 1.2 copy.26
  73.1 0.0 copy-start
  73.1 0.3 fusion
  73.5 0.4 copy.28
  73.9 0.9 all_to_all.15
  74.8 19.3 %all-to-all-start = ((bf16[1024,16,16]{0,2,1:T(8,128)(2,1)}), bf16[1024,16,16]{0,2,1:T(8,128)(2,1)S(1)}, u32[]{:S(2)}, u32[]{:S(2)}) async-start(bf16[1024,16,16]{0,2,1:T(8,128)(2,1)} %all_to_all.15), calls=%async_computation | async-start | bytes 1048576 | tf_op jit(solution)/shard_map/all_to_all | solution.py:59
  94.1 0.0 copy-done
  94.1 0.2 copy.31
  94.3 0.1 reshape.56
  94.5 9.3 %all-to-all-done = bf16[1024,16,16]{0,2,1:T(8,128)(2,1)S(1)} async-done(((bf16[1024,16,16]{0,2,1:T(8,128)(2,1)}), bf16[1024,16,16]{0,2,1:T(8,128)(2,1)S(1)}, u32[]{:S(2)}, u32[]{:S(2)}) %all-to-all-start) | async-done | bytes 524320 | tf_op jit(solution)/shard_map/all_to_all | solution.py:59
  103.8 0.3 copy.29
  104.1 3.8 %fusion.9 = (bf16[1024,4,64]{0,2,1:T(8,128)(2,1)S(1)}, bf16[1024,4,64]{0,2,1:T(8,128)(2,1)}) fusion(f32[1024,4,64]{0,2,1:T(8,128)S(1)} %bitcast.50, bf16[1024,16,4,4]{0,1,3,2:T(8,128)(2,1)S(1)} %bitcast.47, bf16[4,16,4,64]{3,2,1,0:T(4,128)(2,1)S(1)} %bitcast.54), kind=kOutput, calls=%fused_computation.15 | convolution fusion | flops 53215232 | bytes 2654208 | tf_op jit(solution)/shard_map/tpmj,mpjn->tmn/dot_general | solution.py:62
  107.8 0.3 convolution_convert_fusion
  108.1 1.1 copy.33
  109.2 4.6 %all-to-all-start.1 = ((bf16[1024,16,16]{0,2,1:T(8,128)(2,1)}), bf16[1024,16,16]{0,2,1:T(8,128)(2,1)S(1)}, u32[]{:S(2)}, u32[]{:S(2)}) async-start(bf16[1024,16,16]{0,2,1:T(8,128)(2,1)} %copy.33), calls=%async_computation.1 | async-start | bytes 1048576 | tf_op jit(solution)/shard_map/all_to_all | solution.py:75
  113.8 0.3 fusion.17
  114.1 0.1 copy.37
  114.1 9.4 %all-to-all-done.1 = bf16[1024,16,16]{0,2,1:T(8,128)(2,1)S(1)} async-done(((bf16[1024,16,16]{0,2,1:T(8,128)(2,1)}), bf16[1024,16,16]{0,2,1:T(8,128)(2,1)S(1)}, u32[]{:S(2)}, u32[]{:S(2)}) %all-to-all-start.1) | async-done | bytes 524320 | tf_op jit(solution)/shard_map/all_to_all | solution.py:75
  123.5 0.3 copy.34
  123.8 0.3 convolution_bitcast_fusion.1
  124.1 1.0 copy.36
  125.1 0.0 copy-start.1
  125.1 1.0 concatenate.12
  126.2 0.1 maximum_bitcast_fusion
  126.3 0.1 copy.38
  126.4 0.9 reshape.68
  127.3 3.9 %all-to-all-start.2 = ((f32[32,1,1024]{2,1,0:T(1,128)}), f32[32,1,1024]{2,1,0:T(1,128)S(1)}, u32[]{:S(2)}, u32[]{:S(2)}) async-start(f32[32,1,1024]{2,1,0:T(1,128)} %reshape.68), calls=%async_computation.2 | async-start | bytes 262144 | tf_op jit(solution)/shard_map/all_to_all | solution.py:33
  131.2 0.0 copy-done.1
  131.2 1.0 copy.39
  132.2 15.5 %all-to-all-done.2 = f32[32,1,1024]{2,1,0:T(1,128)S(1)} async-done(((f32[32,1,1024]{2,1,0:T(1,128)}), f32[32,1,1024]{2,1,0:T(1,128)S(1)}, u32[]{:S(2)}, u32[]{:S(2)}) %all-to-all-start.2) | async-done | bytes 131104 | tf_op jit(solution)/shard_map/all_to_all | solution.py:33
  147.7 0.5 broadcast.18
  148.2 0.9 reduce
  149.2 0.2 reshape.69
  149.4 0.1 reduce_sum.9
  149.5 0.6 fusion.24
  (5 shorter events, 0.1 us)
Async XLA Ops:
  73.1 21.0 %copy-start = (bf16[1024,256]{1,0:T(8,128)(2,1)S(1)}, bf16[1024,256]{1,0:T(8,128)(2,1)}, u32[]{:S(2)}) copy-start(bf16[1024,256]{1,0:T(8,128)(2,1)} %param.7) | copy-start | bytes 1572868
  74.8 29.0 %all-to-all-start = ((bf16[1024,16,16]{0,2,1:T(8,128)(2,1)}), bf16[1024,16,16]{0,2,1:T(8,128)(2,1)S(1)}, u32[]{:S(2)}, u32[]{:S(2)}) async-start(bf16[1024,16,16]{0,2,1:T(8,128)(2,1)} %all_to_all.15), calls=%async_computation | async-start | bytes 1048576 | tf_op jit(solution)/shard_map/all_to_all | solution.py:59
  109.2 14.3 %all-to-all-start.1 = ((bf16[1024,16,16]{0,2,1:T(8,128)(2,1)}), bf16[1024,16,16]{0,2,1:T(8,128)(2,1)S(1)}, u32[]{:S(2)}, u32[]{:S(2)}) async-start(bf16[1024,16,16]{0,2,1:T(8,128)(2,1)} %copy.33), calls=%async_computation.1 | async-start | bytes 1048576 | tf_op jit(solution)/shard_map/all_to_all | solution.py:75
  125.1 6.1 %copy-start.1 = (bf16[1024,4,64]{0,2,1:T(8,128)(2,1)S(1)}, bf16[1024,4,64]{0,2,1:T(8,128)(2,1)}, u32[]{:S(2)}) copy-start(bf16[1024,4,64]{0,2,1:T(8,128)(2,1)} %get-tuple-element.13) | copy-start | bytes 1572868
  127.3 20.4 %all-to-all-start.2 = ((f32[32,1,1024]{2,1,0:T(1,128)}), f32[32,1,1024]{2,1,0:T(1,128)S(1)}, u32[]{:S(2)}, u32[]{:S(2)}) async-start(f32[32,1,1024]{2,1,0:T(1,128)} %reshape.68), calls=%async_computation.2 | async-start | bytes 262144 | tf_op jit(solution)/shard_map/all_to_all | solution.py:33
where the time goes:
time: 152 us; the launch traced here: 150 us
  blocking collectives  69.5 us (46%)
  waiting for transfers between devices  34.2 us (23%)
  starting transfers between devices  27.7 us (18%)
  local copies, waits for them, and re-layouts  11.7 us (8%)
  matrix products  4.94 us (3%)
    all_gather x1, blocking collectives, gather_together(): lines, at, gathered = (lax.all_gather(line, axis), 0, [])  69.5 us
    all_to_all x1, starting transfers between devices, shards(): lax.all_to_all(inner, 'mp', split_axis=1, concat_axis=1, tiled=True)  19.3 us
    all_to_all x1, waiting for transfers between devices, sent_and_summed(): parts = lax.all_to_all(cut_along(x, dim, devices), axis, 0, 0, tiled=True)  15.5 us
    all_to_all x1, waiting for transfers between devices, shards(): lax.all_to_all(dmixed, 'mp', split_axis=1, concat_axis=1, tiled=True)  9.41 us
    all_to_all x1, waiting for transfers between devices, shards(): lax.all_to_all(inner, 'mp', split_axis=1, concat_axis=1, tiled=True)  9.32 us
    all_to_all x1, starting transfers between devices, shards(): lax.all_to_all(dmixed, 'mp', split_axis=1, concat_axis=1, tiled=True)  4.58 us
    all_to_all x1, starting transfers between devices, sent_and_summed(): parts = lax.all_to_all(cut_along(x, dim, devices), axis, 0, 0, tiled=True)  3.86 us
    dot_general x1, matrix products, shards(): jnp.einsum('tpmj,mpjn->tmn', mixed, left_four, preferred_element_type=jnp...  3.76 us
  transfers between devices with their start and end apart: 3, of which 3 were waited for; matrix products, arithmetic and copies ran while one was open for 1% of the time, Pallas kernels for 0%

commit v1 on v0

--- a/solution.py
+++ b/solution.py
@@ -15,7 +15,10 @@
 
 def gather_together(arrays, axis, dims):
     line = jnp.concatenate([a.reshape(-1) for a in arrays])
-    lines, at, gathered = (lax.all_gather(line, axis), 0, [])
+    devices = lax.axis_size(axis)
+    copies = jnp.broadcast_to(line.reshape(1, -1, 128), (devices, line.size // 128, 128))
+    lines = lax.all_to_all(copies, axis, 0, 0, tiled=True).reshape(devices, -1)
+    at, gathered = (0, [])
     for a, dim in zip(arrays, dims):
         parts = lines[:, at : at + a.size].reshape(-1, *a.shape)
         gathered.append(in_order(parts, dim))

time: 152 us -> 102 us (0.67)
  blocking collectives: 69.5 us -> 0 us
  waiting for transfers between devices: 34.2 us -> 47.7 us
  starting transfers between devices: 27.7 us -> 33.5 us
    all_gather x1 -> x0, blocking collectives: 69.5 us -> none  [gather_together(): lines, at, gathered = (lax.all_gather(line, axis), 0, [])]
    all_to_all x0 -> x1, starting transfers between devices: none -> 18.6 us  [gather_together(): lines = lax.all_to_all(copies, axis, 0, 0, tiled=True).reshape(devices, -1)]
    all_to_all x0 -> x1, waiting for transfers between devices: none -> 13.5 us  [gather_together(): lines = lax.all_to_all(copies, axis, 0, 0, tiled=True).reshape(devices, -1)]
    all_to_all x1, starting transfers between devices: 19.3 us -> 6.4 us  [shards(): lax.all_to_all(inner, 'mp', split_axis=1, concat_axis=1, tiled=True)]
    concatenate x0 -> x2, local copies, waits for them, and re-layouts: none -> 1.53 us  [gather_together(): line = jnp.concatenate([a.reshape(-1) for a in arrays])]
    reshape x2 -> x0, local copies, waits for them, and re-layouts: 1.53 us -> none  [gather_together(): line = jnp.concatenate([a.reshape(-1) for a in arrays])]
    unnamed x8 -> x9, local copies, waits for them, and re-layouts: 3.37 us -> 3.39 us
  transfers between devices with their start and end apart: 3 -> 4, of which waited for: 3 -> 4; matrix products, arithmetic and copies ran while one was open for 1% -> 3% of each run, Pallas kernels for 0% -> 0%
where the time goes in v1:
time: 102 us; the launch traced here: 100 us
  waiting for transfers between devices  47.7 us (47%)
  starting transfers between devices  33.5 us (33%)
  local copies, waits for them, and re-layouts  12.3 us (12%)
  matrix products  4.94 us (5%)
  other arithmetic  1.23 us (1%)
    all_to_all x1, starting transfers between devices, gather_together(): lines = lax.all_to_all(copies, axis, 0, 0, tiled=True).reshape(devices, -1)  18.6 us
    all_to_all x1, waiting for transfers between devices, sent_and_summed(): parts = lax.all_to_all(cut_along(x, dim, devices), axis, 0, 0, tiled=True)  15.5 us
    all_to_all x1, waiting for transfers between devices, gather_together(): lines = lax.all_to_all(copies, axis, 0, 0, tiled=True).reshape(devices, -1)  13.5 us
    all_to_all x1, waiting for transfers between devices, shards(): lax.all_to_all(dmixed, 'mp', split_axis=1, concat_axis=1, tiled=True)  9.4 us
    all_to_all x1, waiting for transfers between devices, shards(): lax.all_to_all(inner, 'mp', split_axis=1, concat_axis=1, tiled=True)  9.32 us
    all_to_all x1, starting transfers between devices, shards(): lax.all_to_all(inner, 'mp', split_axis=1, concat_axis=1, tiled=True)  6.4 us
    all_to_all x1, starting transfers between devices, shards(): lax.all_to_all(dmixed, 'mp', split_axis=1, concat_axis=1, tiled=True)  4.58 us
    all_to_all x1, starting transfers between devices, sent_and_summed(): parts = lax.all_to_all(cut_along(x, dim, devices), axis, 0, 0, tiled=True)  3.84 us
  transfers between devices with their start and end apart: 4, of which 4 were waited for; matrix products, arithmetic and copies ran while one was open for 3% of the time, Pallas kernels for 0%

profile of v1, /device:TPU:1, one launch (start us, length us, event | category | flops | bytes accessed | tf_op | source)
XLA Modules:
  0.0 100.5 jit_solution(8270502554467736325)
XLA Ops:
  0.6 0.8 concatenate.17
  1.4 0.8 concatenate.16
  2.2 0.6 broadcast_in_dim.2
  2.8 18.6 %all-to-all-start = ((bf16[32,8,128]{2,1,0:T(8,128)(2,1)}), bf16[32,8,128]{2,1,0:T(8,128)(2,1)S(1)}, u32[]{:S(2)}, u32[]{:S(2)}) async-start(bf16[32,8,128]{2,1,0:T(8,128)(2,1)} %broadcast_in_dim.2), calls=%async_computation | async-start | bytes 131072 | tf_op jit(solution)/shard_map/all_to_all | solution.py:20
  21.5 1.2 %copy.26 = bf16[1024,256]{0,1:T(8,128)(2,1)S(1)} copy(bf16[1024,256]{1,0:T(8,128)(2,1)} %param.4) | data formatting | bytes 1048576 | tf_op args[0]
  22.7 13.5 %all-to-all-done = bf16[32,8,128]{2,1,0:T(8,128)(2,1)S(1)} async-done(((bf16[32,8,128]{2,1,0:T(8,128)(2,1)}), bf16[32,8,128]{2,1,0:T(8,128)(2,1)S(1)}, u32[]{:S(2)}, u32[]{:S(2)}) %all-to-all-start) | async-done | bytes 65568 | tf_op jit(solution)/shard_map/all_to_all | solution.py:20
  36.2 0.1 reshape.61
  36.4 0.0 copy-start
  36.4 0.3 fusion
  36.7 0.4 copy.28
  37.2 0.9 all_to_all.19
  38.1 6.4 %all-to-all-start.1 = ((bf16[1024,16,16]{0,2,1:T(8,128)(2,1)}), bf16[1024,16,16]{0,2,1:T(8,128)(2,1)S(1)}, u32[]{:S(2)}, u32[]{:S(2)}) async-start(bf16[1024,16,16]{0,2,1:T(8,128)(2,1)} %all_to_all.19), calls=%async_computation.1 | async-start | bytes 1048576 | tf_op jit(solution)/shard_map/all_to_all | solution.py:62
  44.5 0.0 copy-done
  44.5 0.2 copy.31
  44.7 0.1 reshape.60
  44.9 9.3 %all-to-all-done.1 = bf16[1024,16,16]{0,2,1:T(8,128)(2,1)S(1)} async-done(((bf16[1024,16,16]{0,2,1:T(8,128)(2,1)}), bf16[1024,16,16]{0,2,1:T(8,128)(2,1)S(1)}, u32[]{:S(2)}, u32[]{:S(2)}) %all-to-all-start.1) | async-done | bytes 524320 | tf_op jit(solution)/shard_map/all_to_all | solution.py:62
  54.2 0.3 copy.29
  54.5 3.8 %fusion.9 = (bf16[1024,4,64]{0,2,1:T(8,128)(2,1)S(1)}, bf16[1024,4,64]{0,2,1:T(8,128)(2,1)}) fusion(f32[1024,4,64]{0,2,1:T(8,128)S(1)} %bitcast.54, bf16[1024,16,4,4]{0,1,3,2:T(8,128)(2,1)S(1)} %bitcast.51, bf16[4,16,4,64]{3,2,1,0:T(4,128)(2,1)S(1)} %bitcast.58), kind=kOutput, calls=%fused_computation.15 | convolution fusion | flops 53215232 | bytes 2654208 | tf_op jit(solution)/shard_map/tpmj,mpjn->tmn/dot_general | solution.py:65
  58.2 0.3 convolution_convert_fusion
  58.5 1.1 %copy.33 = bf16[1024,16,16]{0,2,1:T(8,128)(2,1)} copy(bf16[1024,16,16]{0,1,2:T(8,128)(2,1)S(1)} %bitcast.53) | data formatting | bytes 1048576 | tf_op jit(solution)/shard_map/all_to_all | solution.py:78
  59.6 4.6 %all-to-all-start.2 = ((bf16[1024,16,16]{0,2,1:T(8,128)(2,1)}), bf16[1024,16,16]{0,2,1:T(8,128)(2,1)S(1)}, u32[]{:S(2)}, u32[]{:S(2)}) async-start(bf16[1024,16,16]{0,2,1:T(8,128)(2,1)} %copy.33), calls=%async_computation.2 | async-start | bytes 1048576 | tf_op jit(solution)/shard_map/all_to_all | solution.py:78
  64.2 0.3 fusion.17
  64.5 0.1 copy.37
  64.5 9.4 %all-to-all-done.2 = bf16[1024,16,16]{0,2,1:T(8,128)(2,1)S(1)} async-done(((bf16[1024,16,16]{0,2,1:T(8,128)(2,1)}), bf16[1024,16,16]{0,2,1:T(8,128)(2,1)S(1)}, u32[]{:S(2)}, u32[]{:S(2)}) %all-to-all-start.2) | async-done | bytes 524320 | tf_op jit(solution)/shard_map/all_to_all | solution.py:78
  73.9 0.3 copy.34
  74.2 0.3 convolution_bitcast_fusion.1
  74.5 1.0 copy.36
  75.5 0.0 copy-start.1
  75.5 1.0 %concatenate.19 = f32[4,32,2,64]{3,2,1,0:T(2,128)S(1)} reshape(f32[4,64,16,4]{3,2,1,0:T(8,128)S(1)} %copy.36) | data formatting | bytes 131072 | tf_op jit(solution)/shard_map/concatenate | solution.py:42
  76.6 0.1 maximum_bitcast_fusion
  76.7 0.1 copy.38
  76.8 0.9 reshape.71
  77.7 3.8 %all-to-all-start.3 = ((f32[32,1,1024]{2,1,0:T(1,128)}), f32[32,1,1024]{2,1,0:T(1,128)S(1)}, u32[]{:S(2)}, u32[]{:S(2)}) async-start(f32[32,1,1024]{2,1,0:T(1,128)} %reshape.71), calls=%async_computation.3 | async-start | bytes 262144 | tf_op jit(solution)/shard_map/all_to_all | solution.py:36
  81.6 0.0 copy-done.1
  81.6 1.0 copy.39
  82.6 15.5 %all-to-all-done.3 = f32[32,1,1024]{2,1,0:T(1,128)S(1)} async-done(((f32[32,1,1024]{2,1,0:T(1,128)}), f32[32,1,1024]{2,1,0:T(1,128)S(1)}, u32[]{:S(2)}, u32[]{:S(2)}) %all-to-all-start.3) | async-done | bytes 131104 | tf_op jit(solution)/shard_map/all_to_all | solution.py:36
  98.1 0.5 broadcast.18
  98.6 0.9 reduce
  99.5 0.2 reshape.72
  99.7 0.1 reduce_sum.9
  99.9 0.6 fusion.24
  (5 shorter events, 0.1 us)
Async XLA Ops:
  2.8 33.4 %all-to-all-start = ((bf16[32,8,128]{2,1,0:T(8,128)(2,1)}), bf16[32,8,128]{2,1,0:T(8,128)(2,1)S(1)}, u32[]{:S(2)}, u32[]{:S(2)}) async-start(bf16[32,8,128]{2,1,0:T(8,128)(2,1)} %broadcast_in_dim.2), calls=%async_computation | async-start | bytes 131072 | tf_op jit(solution)/shard_map/all_to_all | solution.py:20
  36.4 8.1 %copy-start = (bf16[1024,256]{1,0:T(8,128)(2,1)S(1)}, bf16[1024,256]{1,0:T(8,128)(2,1)}, u32[]{:S(2)}) copy-start(bf16[1024,256]{1,0:T(8,128)(2,1)} %param.7) | copy-start | bytes 1572868
  38.1 16.1 %all-to-all-start.1 = ((bf16[1024,16,16]{0,2,1:T(8,128)(2,1)}), bf16[1024,16,16]{0,2,1:T(8,128)(2,1)S(1)}, u32[]{:S(2)}, u32[]{:S(2)}) async-start(bf16[1024,16,16]{0,2,1:T(8,128)(2,1)} %all_to_all.19), calls=%async_computation.1 | async-start | bytes 1048576 | tf_op jit(solution)/shard_map/all_to_all | solution.py:62
  59.6 14.3 %all-to-all-start.2 = ((bf16[1024,16,16]{0,2,1:T(8,128)(2,1)}), bf16[1024,16,16]{0,2,1:T(8,128)(2,1)S(1)}, u32[]{:S(2)}, u32[]{:S(2)}) async-start(bf16[1024,16,16]{0,2,1:T(8,128)(2,1)} %copy.33), calls=%async_computation.2 | async-start | bytes 1048576 | tf_op jit(solution)/shard_map/all_to_all | solution.py:78
  75.5 6.1 %copy-start.1 = (bf16[1024,4,64]{0,2,1:T(8,128)(2,1)S(1)}, bf16[1024,4,64]{0,2,1:T(8,128)(2,1)}, u32[]{:S(2)}) copy-start(bf16[1024,4,64]{0,2,1:T(8,128)(2,1)} %get-tuple-element.13) | copy-start | bytes 1572868
  77.7 20.3 %all-to-all-start.3 = ((f32[32,1,1024]{2,1,0:T(1,128)}), f32[32,1,1024]{2,1,0:T(1,128)S(1)}, u32[]{:S(2)}, u32[]{:S(2)}) async-start(f32[32,1,1024]{2,1,0:T(1,128)} %reshape.71), calls=%async_computation.3 | async-start | bytes 262144 | tf_op jit(solution)/shard_map/all_to_all | solution.py:36

commit v2 on v0

v2 whole, which is shorter than its diff:
```python
import jax
import jax.numpy as jnp
import numpy as np
from jax import lax
from jax.sharding import PartitionSpec as P

NB = 64
BS = 64
F32, BF16 = jnp.float32, jnp.bfloat16
DP_FIRST = 24
MP_FIRST = 9


def order(size, first):
    return [(first + j) % size for j in range(size)]


def exchange(x, axis, members):
    return lax.all_to_all(x, axis, 0, 0, axis_index_groups=[members], tiled=True)


def dot(a, b, ca, cb):
    return lax.dot_general(a, b, (((ca,), (cb,)), ((), ())), preferred_element_type=F32)


def shards(tokens, right_weight, left_weight, cotangent):
    rows = tokens.shape[0]
    groups, n_dp = lax.axis_size("mp"), lax.axis_size("dp")
    owned, held = NB // groups, right_weight.shape[1]
    width = owned * BS
    dps, mps = order(n_dp, DP_FIRST % n_dp), order(groups, MP_FIRST % groups)

    mine = jnp.concatenate([right_weight, left_weight], axis=2)
    lines = exchange(jnp.broadcast_to(mine, (n_dp, *mine.shape)), "dp", dps)
    lines = jnp.roll(lines, dps[0], axis=0)
    right_rows = jnp.moveaxis(lines[..., :BS], 0, 1).reshape(width, BS)
    left_rows = jnp.moveaxis(lines[..., BS:], 0, 1).reshape(owned, NB, BS)

    column = np.arange(width)
    target = np.asarray(mps)[column // (owned * owned)] * owned + column % owned
    block = (column // owned) % owned
    spread = jnp.asarray(target)[None, :] == jnp.arange(BS)[:, None]
    own_block = jnp.arange(width)[:, None] // BS == jnp.asarray(block)[None, :]
    wide = dot(right_rows, spread.astype(BF16), 1, 0)
    right_wide = jnp.where(own_block, wide, 0.0).astype(BF16)

    inner = dot(right_wide, tokens, 0, 1).astype(BF16)
    inner = exchange(inner.reshape(groups, -1, rows), "mp", mps).reshape(width, rows)

    left_by_i = jnp.roll(jnp.moveaxis(left_rows, 1, 0), -mps[0] * owned, axis=0)
    eye = jnp.eye(owned, dtype=BF16)
    left_wide = (left_by_i[:, None] * eye[None, :, :, None]).reshape(width, width)

    pre = dot(inner, left_wide, 0, 0)
    cdf = 0.5 * (1.0 + lax.erf(pre * 0.7071067811865476))
    density = jnp.exp(-0.5 * pre * pre) * 0.3989422804014327
    activated = (pre * cdf).astype(BF16)
    dpre = (cotangent.astype(F32) * (cdf + pre * density)).astype(BF16)

    dmixed = dot(left_wide, dpre, 1, 1).astype(BF16)
    dinner = exchange(dmixed.reshape(groups, -1, rows), "mp", mps).reshape(width, rows)

    part_left = dot(inner, dpre, 1, 0).reshape(NB, owned, owned, BS)
    part_left = jnp.sum(part_left * eye.astype(F32)[None, :, :, None], axis=2).astype(BF16)
    part_left = jnp.roll(part_left, mps[0] * owned, axis=0)
    part_left = part_left.reshape(n_dp, held, owned, BS).swapaxes(1, 2)

    part_right = dot(tokens, dinner, 0, 1)
    part_right = jnp.where(own_block, part_right, 0.0).astype(BF16)
    part_right = dot(part_right, spread.astype(BF16), 1, 1).astype(BF16)
    part_right = jnp.moveaxis(part_right.reshape(owned, n_dp, held, BS), 1, 0)

    parts = jnp.roll(jnp.concatenate([part_right, part_left], axis=3), -dps[0], axis=0)
    sums = jnp.sum(exchange(parts, "dp", dps).astype(F32), axis=0)
    return (activated, sums[..., :BS], sums[..., BS:])


def solution(mesh):
    return jax.shard_map(
        shards,
        mesh=mesh,
        in_specs=(P("dp", "mp"), P("mp", "dp", None), P("mp", "dp", None), P("dp", "mp")),
        out_specs=(P("dp", "mp"), P("mp", "dp", None), P("mp", "dp", None)),
        check_vma=False,
    )
```

time: 152 us -> 81.8 us (0.54)
  blocking collectives: 69.5 us -> 0 us
  starting transfers between devices: 27.7 us -> 49.9 us
  waiting for transfers between devices: 34.2 us -> 20.5 us
  local copies, waits for them, and re-layouts: 11.7 us -> 4.66 us
    all_gather x1 -> x0, blocking collectives: 69.5 us -> none  [gather_together(): lines, at, gathered = (lax.all_gather(line, axis), 0, [])]
    all_to_all x3 -> x4, starting transfers between devices: 27.7 us -> 49.9 us  [exchange(): lax.all_to_all(x, axis, 0, 0, axis_index_groups=[members], tiled=True)]
    all_to_all x3 -> x4, waiting for transfers between devices: 34.2 us -> 20.5 us  [exchange(): lax.all_to_all(x, axis, 0, 0, axis_index_groups=[members], tiled=True)]
    all_to_all x5 -> x0, local copies, waits for them, and re-layouts: 3.09 us -> none  [the longest x2 1.37 us: shards(): lax.all_to_all(dmixed, 'mp', split_axis=1, concat_axis=1, tiled=True)]
    reshape x5 -> x0, local copies, waits for them, and re-layouts: 1.78 us -> none  [the longest x2 1.53 us: gather_together(): line = jnp.concatenate([a.reshape(-1) for a in arrays])]
    unnamed x8 -> x10, local copies, waits for them, and re-layouts: 3.37 us -> 1.89 us
  transfers between devices with their start and end apart: 3 -> 4, of which waited for: 3 -> 4; matrix products, arithmetic and copies ran while one was open for 1% -> 3% of each run, Pallas kernels for 0% -> 0%
where the time goes in v2:
time: 81.8 us; the launch traced here: 81.4 us
  starting transfers between devices  49.9 us (61%)
  waiting for transfers between devices  20.5 us (25%)
  local copies, waits for them, and re-layouts  4.66 us (6%)
  matrix products  4.06 us (5%)
  other arithmetic  1.48 us (2%)
  between operations  0.84 us (1%)
    all_to_all x4, starting transfers between devices, exchange(): lax.all_to_all(x, axis, 0, 0, axis_index_groups=[members], tiled=True)  49.9 us
    all_to_all x4, waiting for transfers between devices, exchange(): lax.all_to_all(x, axis, 0, 0, axis_index_groups=[members], tiled=True)  20.5 us
    dot_general x5, matrix products, dot(): lax.dot_general(a, b, (((ca,), (cb,)), ((), ())), preferred_element_type=...  4.06 us
    unnamed x10, local copies, waits for them, and re-layouts  1.89 us
  transfers between devices with their start and end apart: 4, of which 4 were waited for; matrix products, arithmetic and copies ran while one was open for 3% of the time, Pallas kernels for 0%

profile of v2, /device:TPU:1, one launch (start us, length us, event | category | flops | bytes accessed | tf_op | source)
XLA Modules:
  0.0 81.4 jit_solution(12679328594480005959)
XLA Ops:
  0.6 0.0 copy-start
  0.6 0.8 %pad_maximum_fusion.5 = bf16[4,2,128]{2,1,0:T(2,128)(2,1)S(1)} fusion(bf16[4,2,64]{2,1,0:T(2,128)(2,1)} %param.8, bf16[4,2,64]{2,1,0:T(2,128)(2,1)} %param.7), kind=kLoop, calls=%fused_computation.42 | loop fusion | flops 4096 | bytes 4096 | tf_op jit(solution)/shard_map/concatenate | solution.py:33
  1.5 0.7 broadcast_in_dim.7
  2.1 21.9 %all-to-all-start = ((bf16[32,4,2,128]{3,2,1,0:T(2,128)(2,1)}), bf16[32,4,2,128]{3,2,1,0:T(2,128)(2,1)S(1)}, u32[]{:S(2)}, u32[]{:S(2)}) async-start(bf16[32,4,2,128]{3,2,1,0:T(2,128)(2,1)} %broadcast_in_dim.7), calls=%async_computation | async-start | bytes 131072 | tf_op jit(solution)/shard_map/all_to_all | solution.py:19
  24.1 3.0 %all-to-all-done = bf16[32,4,2,128]{3,2,1,0:T(2,128)(2,1)S(1)} async-done(((bf16[32,4,2,128]{3,2,1,0:T(2,128)(2,1)}), bf16[32,4,2,128]{3,2,1,0:T(2,128)(2,1)S(1)}, u32[]{:S(2)}, u32[]{:S(2)}) %all-to-all-start) | async-done | bytes 65568 | tf_op jit(solution)/shard_map/all_to_all | solution.py:19
  27.1 0.2 fusion.22
  27.3 0.0 copy-start.3
  27.4 0.0 copy-start.2
  27.4 0.0 copy-done
  27.4 0.6 copy-done.3
  28.0 0.1 copy-done.2
  28.0 1.3 %convolution_convert_fusion.1 = bf16[256,1024]{1,0:T(8,128)(2,1)} fusion(bf16[1024,256]{1,0:T(8,128)(2,1)S(1)} %copy-done, bf16[256,64]{1,0:T(8,128)(2,1)S(1)} %bitcast.51, s32[256]{0:T(256)S(1)} %copy-done.3, s32[256]{0:T(256)S(1)} %and_select_fusion, s32[256]{0:T(256)S(1)} %copy-done.2), kind=kOutput, calls=%fused_computation.2 | convolution fusion | flops 143081472 | bytes 1084416 | tf_op jit(solution)/shard_map/dot_general | solution.py:23
  29.4 0.0 copy-start.1
  29.4 7.5 %all-to-all-start.1 = ((bf16[16,16,1024]{2,1,0:T(8,128)(2,1)}), bf16[16,16,1024]{2,1,0:T(8,128)(2,1)S(1)}, u32[]{:S(2)}, u32[]{:S(2)}) async-start(bf16[16,16,1024]{2,1,0:T(8,128)(2,1)} %bitcast.2), calls=%async_computation.1 | async-start | bytes 1048576 | tf_op jit(solution)/shard_map/all_to_all | solution.py:19
  36.9 0.0 copy-done.1
  36.9 0.2 copy.20
  37.2 0.1 copy.19
  37.3 0.2 broadcast_multiply_fusion
  37.5 0.2 mul.71
  37.7 7.1 %all-to-all-done.1 = bf16[16,16,1024]{2,1,0:T(8,128)(2,1)S(1)} async-done(((bf16[16,16,1024]{2,1,0:T(8,128)(2,1)}), bf16[16,16,1024]{2,1,0:T(8,128)(2,1)S(1)}, u32[]{:S(2)}, u32[]{:S(2)}) %all-to-all-start.1) | async-done | bytes 524320 | tf_op jit(solution)/shard_map/all_to_all | solution.py:19
  44.8 0.7 fusion.11
  45.5 1.1 %convolution_convert_fusion = bf16[256,1024]{1,0:T(8,128)(2,1)} fusion(bf16[256,256]{1,0:T(8,128)(2,1)S(1)} %mul.71, bf16[1024,256]{0,1:T(8,128)(2,1)S(1)} %get-tuple-element.12), kind=kOutput, calls=%fused_computation.1 | convolution fusion | flops 134479872 | bytes 1179648 | tf_op jit(solution)/shard_map/dot_general | solution.py:23
  46.6 5.3 %all-to-all-start.2 = ((bf16[16,16,1024]{2,1,0:T(8,128)(2,1)}), bf16[16,16,1024]{2,1,0:T(8,128)(2,1)S(1)}, u32[]{:S(2)}, u32[]{:S(2)}) async-start(bf16[16,16,1024]{2,1,0:T(8,128)(2,1)} %bitcast.8), calls=%async_computation.2 | async-start | bytes 1048576 | tf_op jit(solution)/shard_map/all_to_all | solution.py:19
  51.9 0.2 dot_general.36
  52.1 0.5 fusion
  52.7 7.5 %all-to-all-done.2 = bf16[16,16,1024]{2,1,0:T(8,128)(2,1)S(1)} async-done(((bf16[16,16,1024]{2,1,0:T(8,128)(2,1)}), bf16[16,16,1024]{2,1,0:T(8,128)(2,1)S(1)}, u32[]{:S(2)}, u32[]{:S(2)}) %all-to-all-start.2) | async-done | bytes 524320 | tf_op jit(solution)/shard_map/all_to_all | solution.py:19
  60.2 0.5 fusion.5
  60.6 0.1 copy.22
  60.8 0.2 fusion.21
  60.9 0.7 copy.24
  61.6 15.1 %all-to-all-start.3 = ((bf16[32,4,2,128]{3,2,1,0:T(2,128)(2,1)}), bf16[32,4,2,128]{3,2,1,0:T(2,128)(2,1)S(1)}, u32[]{:S(2)}, u32[]{:S(2)}) async-start(bf16[32,4,2,128]{3,2,1,0:T(2,128)(2,1)} %copy.24), calls=%async_computation.3 | async-start | bytes 131072 | tf_op jit(solution)/shard_map/all_to_all | solution.py:19
  76.7 1.0 %copy.25 = bf16[1024,256]{1,0:T(8,128)(2,1)} copy(bf16[1024,256]{0,1:T(8,128)(2,1)S(1)} %get-tuple-element.13) | data formatting | bytes 1048576
  77.7 2.9 %all-to-all-done.3 = bf16[32,4,2,128]{3,2,1,0:T(2,128)(2,1)S(1)} async-done(((bf16[32,4,2,128]{3,2,1,0:T(2,128)(2,1)}), bf16[32,4,2,128]{3,2,1,0:T(2,128)(2,1)S(1)}, u32[]{:S(2)}, u32[]{:S(2)}) %all-to-all-start.3) | async-done | bytes 65568 | tf_op jit(solution)/shard_map/all_to_all | solution.py:19
  80.6 0.1 convert_reduce_fusion
  80.7 0.7 fusion.30
  (13 shorter events, 0.2 us)
Async XLA Ops:
  0.6 26.7 %copy-start = (bf16[1024,256]{1,0:T(8,128)(2,1)S(1)}, bf16[1024,256]{1,0:T(8,128)(2,1)}, u32[]{:S(2)}) copy-start(bf16[1024,256]{1,0:T(8,128)(2,1)} %param.6) | copy-start | bytes 1572868
  2.1 24.9 %all-to-all-start = ((bf16[32,4,2,128]{3,2,1,0:T(2,128)(2,1)}), bf16[32,4,2,128]{3,2,1,0:T(2,128)(2,1)S(1)}, u32[]{:S(2)}, u32[]{:S(2)}) async-start(bf16[32,4,2,128]{3,2,1,0:T(2,128)(2,1)} %broadcast_in_dim.7), calls=%async_computation | async-start | bytes 131072 | tf_op jit(solution)/shard_map/all_to_all | solution.py:19
  27.3 0.7 copy-start.3
  27.4 0.7 copy-start.2
  29.4 7.5 %copy-start.1 = (bf16[1024,256]{1,0:T(8,128)(2,1)S(1)}, bf16[1024,256]{1,0:T(8,128)(2,1)}, u32[]{:S(2)}) copy-start(bf16[1024,256]{1,0:T(8,128)(2,1)} %param.9) | copy-start | bytes 1572868
  29.4 15.4 %all-to-all-start.1 = ((bf16[16,16,1024]{2,1,0:T(8,128)(2,1)}), bf16[16,16,1024]{2,1,0:T(8,128)(2,1)S(1)}, u32[]{:S(2)}, u32[]{:S(2)}) async-start(bf16[16,16,1024]{2,1,0:T(8,128)(2,1)} %bitcast.2), calls=%async_computation.1 | async-start | bytes 1048576 | tf_op jit(solution)/shard_map/all_to_all | solution.py:19
  46.6 13.5 %all-to-all-start.2 = ((bf16[16,16,1024]{2,1,0:T(8,128)(2,1)}), bf16[16,16,1024]{2,1,0:T(8,128)(2,1)S(1)}, u32[]{:S(2)}, u32[]{:S(2)}) async-start(bf16[16,16,1024]{2,1,0:T(8,128)(2,1)} %bitcast.8), calls=%async_computation.2 | async-start | bytes 1048576 | tf_op jit(solution)/shard_map/all_to_all | solution.py:19
  61.6 19.0 %all-to-all-start.3 = ((bf16[32,4,2,128]{3,2,1,0:T(2,128)(2,1)}), bf16[32,4,2,128]{3,2,1,0:T(2,128)(2,1)S(1)}, u32[]{:S(2)}, u32[]{:S(2)}) async-start(bf16[32,4,2,128]{3,2,1,0:T(2,128)(2,1)} %copy.24), calls=%async_computation.3 | async-start | bytes 131072 | tf_op jit(solution)/shard_map/all_to_all | solution.py:19

commit v3 on v2

v3 whole, which is shorter than its diff:
```python
import functools

import jax
import jax.numpy as jnp
from jax import lax
from jax.experimental import pallas as pl
from jax.experimental.pallas import tpu as pltpu
from jax.sharding import PartitionSpec as P

NB = 64
BS = 64
F32, BF16 = jnp.float32, jnp.bfloat16
DP_FIRST = 24
MP_FIRST = 9
STEP = 256


def exchange(x, axis, first):
    size = lax.axis_size(axis)
    members = [(first + j) % size for j in range(size)]
    return lax.all_to_all(x, axis, 0, 0, axis_index_groups=[members], tiled=True)


def dot(a, b, ca, cb):
    return lax.dot_general(a, b, (((ca,), (cb,)), ((), ())), preferred_element_type=F32)


def where(rows, columns, test):
    r = lax.broadcasted_iota(jnp.int32, (rows, columns), 0)
    c = lax.broadcasted_iota(jnp.int32, (rows, columns), 1)
    return test(r, c)


def one_hot(rows, columns, test):
    return jnp.where(where(rows, columns, test), 1.0, 0.0).astype(BF16)


class Plan:
    def __init__(self, groups, n_dp, held):
        self.groups, self.n_dp, self.held = groups, n_dp, held
        self.owned = NB // groups
        self.width = self.owned * BS

    def peer_m(self, r):
        return r // self.held % self.owned

    def peer_i(self, r):
        chunk = self.owned * self.owned
        return r % chunk // (self.owned * self.held) * self.held + r % self.held

    def target(self, r):
        peer = (r // (self.owned * self.owned) + MP_FIRST) % self.groups
        return peer * self.owned + self.peer_m(r)

    def line_feature(self, r):
        line = self.owned * self.held
        member = (r // line + DP_FIRST) % self.n_dp
        return r % line // self.held * BS + member * self.held + r % self.held

    def spread(self):
        return one_hot(self.width, 2 * BS, lambda r, c: self.target(r) == c)

    def features(self):
        return one_hot(self.width, self.width, lambda r, c: self.line_feature(r) == c)

    def own_block(self, x):
        own = where(self.width, self.width, lambda r, c: self.peer_i(r) == c // BS)
        return jnp.where(own, x, 0.0).astype(BF16)

    def tiles(self):
        return one_hot(2 * BS, self.width, lambda n, c: n == c % BS + BS)

    def own_m(self, x):
        own = where(self.width, self.width, lambda r, c: self.peer_m(r) == c // BS)
        return jnp.where(own, x, 0.0).astype(BF16)

    def turn(self, x, back):
        line = self.owned * self.held
        by = (MP_FIRST * self.owned * self.owned - DP_FIRST * line) % self.width
        by = self.width - by if back else by
        return jnp.concatenate([x[by:], x[:by]], axis=0) if by else x


def first_kernel(plan, lines, tokens, inner):
    right = dot(plan.spread(), lines[...], 1, 1).astype(BF16)
    right = plan.own_block(dot(right, plan.features(), 1, 0))
    inner[...] = dot(right, tokens[...], 1, 1).astype(BF16)


def middle_kernel(plan, lines, inner, cotangent, dmixed, part_left, activated, act, sems):
    left = plan.own_m(dot(plan.turn(lines[...], False), plan.tiles(), 1, 0))
    steps = inner.shape[1] // STEP
    total = None
    copies = []
    for s in range(steps):
        at = pl.ds(s * STEP, STEP)
        some = inner[:, at]
        pre = dot(some, left, 0, 0)
        cdf = 0.5 * (1.0 + lax.erf(pre * 0.7071067811865476))
        density = jnp.exp(-0.5 * pre * pre) * 0.3989422804014327
        act[at, :] = (pre * cdf).astype(BF16)
        copies.append(pltpu.make_async_copy(act.at[at, :], activated.at[at, :], sems.at[s]))
        copies[-1].start()
        dpre = (cotangent[at, :].astype(F32) * (cdf + pre * density)).astype(BF16)
        dmixed[:, at] = dot(left, dpre, 1, 1).astype(BF16)
        part = dot(some, dpre, 1, 0)
        total = part if total is None else total + part
    part_left[...] = plan.turn(dot(plan.own_m(total), plan.tiles(), 1, 1), True).astype(BF16)
    for copy in copies:
        copy.wait()


def last_kernel(plan, dinner, tokens, part_left, parts):
    part = plan.own_block(dot(dinner[...], tokens[...], 1, 0))
    part = dot(plan.spread(), part, 0, 0).astype(BF16)
    parts[...] = (dot(plan.features(), part, 1, 1) + part_left[...].astype(F32)).astype(BF16)


VMEM = pl.BlockSpec(memory_space=pltpu.VMEM)
PARAMS = pltpu.CompilerParams(vmem_limit_bytes=24 * 1024 * 1024)


def shards(tokens, right_weight, left_weight, cotangent):
    rows = tokens.shape[0]
    groups, n_dp = lax.axis_size("mp"), lax.axis_size("dp")
    plan = Plan(groups, n_dp, right_weight.shape[1])
    width = plan.width

    mine = jnp.concatenate([right_weight, left_weight], axis=2)
    lines = exchange(jnp.broadcast_to(mine, (n_dp, *mine.shape)), "dp", DP_FIRST)
    lines = lines.reshape(width, 2 * BS)

    inner = pl.pallas_call(
        functools.partial(first_kernel, plan),
        out_shape=jax.ShapeDtypeStruct((width, rows), BF16),
        in_specs=[VMEM] * 2,
        out_specs=VMEM,
        compiler_params=PARAMS,
    )(lines, tokens)
    inner = exchange(inner.reshape(groups, -1, rows), "mp", MP_FIRST).reshape(width, rows)

    dmixed, part_left, activated = pl.pallas_call(
        functools.partial(middle_kernel, plan),
        out_shape=(
            jax.ShapeDtypeStruct((width, rows), BF16),
            jax.ShapeDtypeStruct((width, 2 * BS), BF16),
            jax.ShapeDtypeStruct((rows, width), BF16),
        ),
        in_specs=[VMEM] * 3,
        out_specs=(VMEM, VMEM, pl.BlockSpec(memory_space=pl.ANY)),
        scratch_shapes=[pltpu.VMEM((rows, width), BF16), pltpu.SemaphoreType.DMA((rows // STEP,))],
        compiler_params=PARAMS,
    )(lines, inner, cotangent)
    dinner = exchange(dmixed.reshape(groups, -1, rows), "mp", MP_FIRST).reshape(width, rows)

    parts = pl.pallas_call(
        functools.partial(last_kernel, plan),
        out_shape=jax.ShapeDtypeStruct((width, 2 * BS), BF16),
        in_specs=[VMEM] * 3,
        out_specs=VMEM,
        compiler_params=PARAMS,
    )(dinner, tokens, part_left)
    sums = jnp.sum(exchange(parts.reshape(n_dp, *mine.shape), "dp", DP_FIRST).astype(F32), axis=0)
    return (activated, sums[..., :BS], sums[..., BS:])


def solution(mesh):
    return jax.shard_map(
        shards,
        mesh=mesh,
        in_specs=(P("dp", "mp"), P("mp", "dp", None), P("mp", "dp", None), P("dp", "mp")),
        out_specs=(P("dp", "mp"), P("mp", "dp", None), P("mp", "dp", None)),
        check_vma=False,
    )
```

time: 81.8 us -> 77.3 us (0.945)
  blocking collectives: 0 us -> 70.2 us
  starting transfers between devices: 49.9 us -> 0 us
  waiting for transfers between devices: 20.5 us -> 0 us
  matrix products: 4.06 us -> 0 us
  Pallas kernels: 0 us -> 3.23 us
  local copies, waits for them, and re-layouts: 4.66 us -> 1.76 us
    all_to_all x0 -> x4, blocking collectives: none -> 70.2 us  [exchange(): lax.all_to_all(x, axis, 0, 0, axis_index_groups=[members], tiled=True)]
    all_to_all x4 -> x0, starting transfers between devices: 49.9 us -> none  [exchange(): lax.all_to_all(x, axis, 0, 0, axis_index_groups=[members], tiled=True)]
    all_to_all x4 -> x0, waiting for transfers between devices: 20.5 us -> none  [exchange(): lax.all_to_all(x, axis, 0, 0, axis_index_groups=[members], tiled=True)]
    dot_general x5 -> x0, matrix products: 4.06 us -> none  [dot(): lax.dot_general(a, b, (((ca,), (cb,)), ((), ())), preferred_element_type=...]
    pallas_call x0 -> x3, Pallas kernels: none -> 3.23 us  [the longest x1 1.97 us: shards(): pl.pallas_call(functools.partial(middle_kernel, plan), out_shape=(jax.Sha...]
    unnamed x10 -> x6, local copies, waits for them, and re-layouts: 1.89 us -> 1.05 us
  transfers between devices with their start and end apart: 4 -> 0, of which waited for: 4 -> 0; matrix products, arithmetic and copies ran while one was open for 3% -> 0% of each run, Pallas kernels for 0% -> 0%
where the time goes in v3:
time: 77.3 us; the launch traced here: 76.7 us
  blocking collectives  70.2 us (91%)
  Pallas kernels  3.23 us (4%)
  local copies, waits for them, and re-layouts  1.76 us (2%)
  other arithmetic  0.85 us (1%)
    all_to_all x4, blocking collectives, exchange(): lax.all_to_all(x, axis, 0, 0, axis_index_groups=[members], tiled=True)  70.2 us
    pallas_call x1, Pallas kernels, shards(): pl.pallas_call(functools.partial(middle_kernel, plan), out_shape=(jax.Sha...  1.97 us

profile of v3, /device:TPU:1, one launch (start us, length us, event | category | flops | bytes accessed | tf_op | source)
XLA Modules:
  0.0 76.7 jit_solution(2634791601280127476)
XLA Ops:
  0.6 0.8 %pad_maximum_fusion = bf16[4,2,128]{2,1,0:T(2,128)(2,1)S(1)} fusion(bf16[4,2,64]{2,1,0:T(2,128)(2,1)} %param.6, bf16[4,2,64]{2,1,0:T(2,128)(2,1)} %param.5), kind=kLoop, calls=%fused_computation.1 | loop fusion | flops 4096 | bytes 4096 | tf_op jit(solution)/shard_map/concatenate | solution.py:129
  1.5 24.7 %all_to_all.20 = bf16[32,4,2,128]{3,2,1,0:T(2,128)(2,1)S(1)} all-to-all(bf16[32,4,2,128]{3,2,1,0:T(2,128)(2,1)S(1)} %broadcast_in_dim.3), channel_id=1, replica_groups={{384,400,416,432,448,464,480,496,0,16,32,48,64,80,96,112,128,144,160,17..., dimensions={0} | all-to-all | bytes 131072 | tf_op jit(solution)/shard_map/all_to_all | solution.py:21
  26.2 0.0 copy-start
  26.2 1.0 %copy-done = bf16[1024,256]{1,0:T(8,128)(2,1)S(1)} copy-done((bf16[1024,256]{1,0:T(8,128)(2,1)S(1)}, bf16[1024,256]{1,0:T(8,128)(2,1)}, u32[]{:S(2)}) %copy-start) | copy-done | bytes 524312
  27.2 0.6 shard_map.67
  27.8 0.0 copy-start.2
  27.8 15.2 %all_to_all.21 = bf16[16,16,1024]{2,1,0:T(8,128)(2,1)S(1)} all-to-all(bf16[16,16,1024]{2,1,0:T(8,128)(2,1)S(1)} %bitcast.8), channel_id=1, replica_groups={{9,10,11,12,13,14,15,0,1,2,3,4,5,6,7,8},{25,26,27,28,29,30,31,16,17,18,..., dimensions={0} | all-to-all | bytes 1048576 | tf_op jit(solution)/shard_map/all_to_all | solution.py:21
  43.0 0.0 copy-done.2
  43.0 2.0 %shard_map.68 = (bf16[256,1024]{1,0:T(8,128)(2,1)S(1)}, bf16[256,128]{1,0:T(8,128)(2,1)S(1)}, bf16[1024,256]{1,0:T(8,128)(2,1)}) custom-call(bf16[256,128]{1,0:T(8,128)(2,1)S(1)} %bitcast.10, bf16[256,1024]{1,0:T(8,128)(2,1)S(1)} %bitcast.6, bf16[1024,256]{1,0:T(8,128)(2,1)S(1)} %copy-done.2), custom_call_target="tpu_custom_call" | custom-call | tf_op jit(solution)/shard_map/pallas_call | solution.py:142
  45.0 0.0 copy-start.1
  45.0 12.7 %all_to_all.22 = bf16[16,16,1024]{2,1,0:T(8,128)(2,1)S(1)} all-to-all(bf16[16,16,1024]{2,1,0:T(8,128)(2,1)S(1)} %bitcast.11), channel_id=1, replica_groups={{9,10,11,12,13,14,15,0,1,2,3,4,5,6,7,8},{25,26,27,28,29,30,31,16,17,18,..., dimensions={0} | all-to-all | bytes 1048576 | tf_op jit(solution)/shard_map/all_to_all | solution.py:21
  57.7 0.0 copy-done.1
  57.7 0.7 shard_map.69
  58.4 17.5 %all_to_all.23 = bf16[32,4,2,128]{3,2,1,0:T(2,128)(2,1)S(1)} all-to-all(bf16[32,4,2,128]{3,2,1,0:T(2,128)(2,1)S(1)} %bitcast.12), channel_id=1, replica_groups={{384,400,416,432,448,464,480,496,0,16,32,48,64,80,96,112,128,144,160,17..., dimensions={0} | all-to-all | bytes 131072 | tf_op jit(solution)/shard_map/all_to_all | solution.py:21
  75.9 0.1 convert_reduce_fusion
  76.0 0.7 fusion
  (1 shorter events, 0.0 us)
Async XLA Ops:
  26.2 1.0 %copy-start = (bf16[1024,256]{1,0:T(8,128)(2,1)S(1)}, bf16[1024,256]{1,0:T(8,128)(2,1)}, u32[]{:S(2)}) copy-start(bf16[1024,256]{1,0:T(8,128)(2,1)} %tokens.3) | copy-start | bytes 1572868
  27.8 15.2 %copy-start.2 = (bf16[1024,256]{1,0:T(8,128)(2,1)S(1)}, bf16[1024,256]{1,0:T(8,128)(2,1)}, u32[]{:S(2)}) copy-start(bf16[1024,256]{1,0:T(8,128)(2,1)} %cotangent.1) | copy-start | bytes 1572868
  45.0 12.7 %copy-start.1 = (bf16[1024,256]{1,0:T(8,128)(2,1)S(1)}, bf16[1024,256]{1,0:T(8,128)(2,1)}, u32[]{:S(2)}) copy-start(bf16[1024,256]{1,0:T(8,128)(2,1)} %tokens.3) | copy-start | bytes 1572868

commit v4 on v3

--- a/solution.py
+++ b/solution.py
@@ -25,14 +25,22 @@
     return lax.dot_general(a, b, (((ca,), (cb,)), ((), ())), preferred_element_type=F32)
 
 
-def where(rows, columns, test):
-    r = lax.broadcasted_iota(jnp.int32, (rows, columns), 0)
-    c = lax.broadcasted_iota(jnp.int32, (rows, columns), 1)
-    return test(r, c)
-
-
-def one_hot(rows, columns, test):
-    return jnp.where(where(rows, columns, test), 1.0, 0.0).astype(BF16)
+def div(x, n):
+    return lax.shift_right_logical(x, jnp.int32(n.bit_length() - 1))
+
+
+def mod(x, n):
+    return x & (n - 1)
+
+
+def equal(rows, columns, of_row, of_column):
+    r = of_row(lax.broadcasted_iota(jnp.int32, (rows, 128), 0))
+    c = of_column(lax.broadcasted_iota(jnp.int32, (1, columns), 1))
+    return jnp.concatenate([r] * (columns // 128), axis=1) == c
+
+
+def one_hot(rows, columns, of_row, of_column):
+    return jnp.where(equal(rows, columns, of_row, of_column), 1.0, 0.0).astype(BF16)
 
 
 class Plan:
@@ -40,38 +48,39 @@
         self.groups, self.n_dp, self.held = groups, n_dp, held
         self.owned = NB // groups
         self.width = self.owned * BS
+        assert all(n & (n - 1) == 0 for n in (groups, n_dp, held))
 
     def peer_m(self, r):
-        return r // self.held % self.owned
+        return mod(div(r, self.held), self.owned)
 
     def peer_i(self, r):
-        chunk = self.owned * self.owned
-        return r % chunk // (self.owned * self.held) * self.held + r % self.held
+        high = div(mod(r, self.owned * self.owned), self.owned * self.held)
+        return high * self.held + mod(r, self.held)
 
     def target(self, r):
-        peer = (r // (self.owned * self.owned) + MP_FIRST) % self.groups
+        peer = mod(div(r, self.owned * self.owned) + MP_FIRST, self.groups)
         return peer * self.owned + self.peer_m(r)
 
     def line_feature(self, r):
         line = self.owned * self.held
-        member = (r // line + DP_FIRST) % self.n_dp
-        return r % line // self.held * BS + member * self.held + r % self.held
+        member = mod(div(r, line) + DP_FIRST, self.n_dp)
+        return div(mod(r, line), self.held) * BS + member * self.held + mod(r, self.held)
 
     def spread(self):
-        return one_hot(self.width, 2 * BS, lambda r, c: self.target(r) == c)
+        return one_hot(self.width, 2 * BS, self.target, lambda c: c)
 
     def features(self):
-        return one_hot(self.width, self.width, lambda r, c: self.line_feature(r) == c)
+        return one_hot(self.width, self.width, self.line_feature, lambda c: c)
 
     def own_block(self, x):
-        own = where(self.width, self.width, lambda r, c: self.peer_i(r) == c // BS)
+        own = equal(self.width, self.width, self.peer_i, lambda c: div(c, BS))
         return jnp.where(own, x, 0.0).astype(BF16)
 
     def tiles(self):
-        return one_hot(2 * BS, self.width, lambda n, c: n == c % BS + BS)
+        return one_hot(2 * BS, self.width, lambda n: n, lambda c: mod(c, BS) + BS)
 
     def own_m(self, x):
-        own = where(self.width, self.width, lambda r, c: self.peer_m(r) == c // BS)
+        own = equal(self.width, self.width, self.peer_m, lambda c: div(c, BS))
         return jnp.where(own, x, 0.0).astype(BF16)
 
     def turn(self, x, back):
@@ -81,6 +90,19 @@
         return jnp.concatenate([x[by:], x[:by]], axis=0) if by else x
 
 
+def load_kernel(right, left, tokens, copies, held, r, l, sems):
+    loads = [
+        pltpu.make_async_copy(a, b, sems.at[k])
+        for k, (a, b) in enumerate(((right, r), (left, l), (tokens, held)))
+    ]
+    for load in loads:
+        load.start()
+    loads[0].wait()
+    loads[1].wait()
+    copies[...] = jnp.broadcast_to(jnp.concatenate([r[...], l[...]], axis=2), copies.shape)
+    loads[2].wait()
+
+
 def first_kernel(plan, lines, tokens, inner):
     right = dot(plan.spread(), lines[...], 1, 1).astype(BF16)
     right = plan.own_block(dot(right, plan.features(), 1, 0))
@@ -90,21 +112,20 @@
 def middle_kernel(plan, lines, inner, cotangent, dmixed, part_left, activated, act, sems):
     left = plan.own_m(dot(plan.turn(lines[...], False), plan.tiles(), 1, 0))
     steps = inner.shape[1] // STEP
-    total = None
-    copies = []
+    copies, dpres = [], []
     for s in range(steps):
         at = pl.ds(s * STEP, STEP)
-        some = inner[:, at]
-        pre = dot(some, left, 0, 0)
+        pre = dot(inner[:, at], left, 0, 0)
         cdf = 0.5 * (1.0 + lax.erf(pre * 0.7071067811865476))
         density = jnp.exp(-0.5 * pre * pre) * 0.3989422804014327
         act[at, :] = (pre * cdf).astype(BF16)
         copies.append(pltpu.make_async_copy(act.at[at, :], activated.at[at, :], sems.at[s]))
         copies[-1].start()
-        dpre = (cotangent[at, :].astype(F32) * (cdf + pre * density)).astype(BF16)
-        dmixed[:, at] = dot(left, dpre, 1, 1).astype(BF16)
-        part = dot(some, dpre, 1, 0)
-        total = part if total is None else total + part
+        slope = cdf + pre * density
+        dpres.append((cotangent[at, :].astype(F32) * slope).astype(BF16))
+    dpre = jnp.concatenate(dpres, axis=0)
+    dmixed[...] = dot(left, dpre, 1, 1).astype(BF16)
+    total = dot(inner[...], dpre, 1, 0)
     part_left[...] = plan.turn(dot(plan.own_m(total), plan.tiles(), 1, 1), True).astype(BF16)
     for copy in copies:
         copy.wait()
@@ -116,6 +137,7 @@
     parts[...] = (dot(plan.features(), part, 1, 1) + part_left[...].astype(F32)).astype(BF16)
 
 
+HBM = pl.BlockSpec(memory_space=pltpu.HBM)
 VMEM = pl.BlockSpec(memory_space=pltpu.VMEM)
 PARAMS = pltpu.CompilerParams(vmem_limit_bytes=24 * 1024 * 1024)
 
@@ -126,8 +148,23 @@
     plan = Plan(groups, n_dp, right_weight.shape[1])
     width = plan.width
 
-    mine = jnp.concatenate([right_weight, left_weight], axis=2)
-    lines = exchange(jnp.broadcast_to(mine, (n_dp, *mine.shape)), "dp", DP_FIRST)
+    line = (*right_weight.shape[:2], 2 * BS)
+    copies, tokens = pl.pallas_call(
+        load_kernel,
+        out_shape=(
+            pltpu.VMEM((n_dp, *line), BF16),
+            pltpu.VMEM(tokens.shape, BF16),
+        ),
+        in_specs=[HBM] * 3,
+        out_specs=(VMEM, VMEM),
+        scratch_shapes=[
+            pltpu.VMEM(right_weight.shape, BF16),
+            pltpu.VMEM(left_weight.shape, BF16),
+            pltpu.SemaphoreType.DMA((3,)),
+        ],
+        compiler_params=pltpu.CompilerParams(vmem_limit_bytes=60 * 1024 * 1024),
+    )(right_weight, left_weight, tokens)
+    lines = exchange(copies, "dp", DP_FIRST)
     lines = lines.reshape(width, 2 * BS)
 
     inner = pl.pallas_call(
@@ -147,7 +184,7 @@
             jax.ShapeDtypeStruct((rows, width), BF16),
         ),
         in_specs=[VMEM] * 3,
-        out_specs=(VMEM, VMEM, pl.BlockSpec(memory_space=pl.ANY)),
+        out_specs=(VMEM, VMEM, HBM),
         scratch_shapes=[pltpu.VMEM((rows, width), BF16), pltpu.SemaphoreType.DMA((rows // STEP,))],
         compiler_params=PARAMS,
     )(lines, inner, cotangent)
@@ -160,7 +197,7 @@
         out_specs=VMEM,
         compiler_params=PARAMS,
     )(dinner, tokens, part_left)
-    sums = jnp.sum(exchange(parts.reshape(n_dp, *mine.shape), "dp", DP_FIRST).astype(F32), axis=0)
+    sums = jnp.sum(exchange(parts.reshape(n_dp, *line), "dp", DP_FIRST).astype(F32), axis=0)
     return (activated, sums[..., :BS], sums[..., BS:])
 
 

time: 77.3 us -> 76 us (0.983)
  local copies, waits for them, and re-layouts: 1.76 us -> 0.68 us
  Pallas kernels: 3.23 us -> 4.02 us
  other arithmetic: 0.85 us -> 0.07 us
    pallas_call x0 -> x1, Pallas kernels: none -> 1.1 us  [shards(): pl.pallas_call(load_kernel, out_shape=(pltpu.VMEM((n_dp, *line), BF16), p...]
    unnamed x6 -> x2, local copies, waits for them, and re-layouts: 1.05 us -> 0.01 us
    concatenate x1 -> x0, other arithmetic: 0.78 us -> none  [shards(): mine = jnp.concatenate([right_weight, left_weight], axis=2)]
where the time goes in v4:
time: 76 us; the launch traced here: 75.5 us
  blocking collectives  70 us (92%)
  Pallas kernels  4.02 us (5%)
    all_to_all x4, blocking collectives, exchange(): lax.all_to_all(x, axis, 0, 0, axis_index_groups=[members], tiled=True)  70 us
    pallas_call x1, Pallas kernels, shards(): pl.pallas_call(functools.partial(middle_kernel, plan), out_shape=(jax.Sha...  1.7 us

profile of v4, /device:TPU:1, one launch (start us, length us, event | category | flops | bytes accessed | tf_op | source)
XLA Modules:
  0.0 75.5 jit_solution(8283156610354316973)
XLA Ops:
  0.6 1.1 %shard_map.67 = (bf16[32,4,2,128]{3,2,1,0:T(2,128)(2,1)S(1)}, bf16[1024,256]{1,0:T(8,128)(2,1)S(1)}) custom-call(bf16[4,2,64]{2,1,0:T(2,128)(2,1)} %right.1, bf16[4,2,64]{2,1,0:T(2,128)(2,1)} %left.1, bf16[1024,256]{1,0:T(8,128)(2,1)} %tokens.1), custom_call_target="tpu_custom_call" | custom-call | tf_op jit(solution)/shard_map/pallas_call | solution.py:152
  1.7 24.7 %all_to_all.20 = bf16[32,4,2,128]{3,2,1,0:T(2,128)(2,1)S(1)} all-to-all(bf16[32,4,2,128]{3,2,1,0:T(2,128)(2,1)S(1)} %get-tuple-element.8), channel_id=1, replica_groups={{384,400,416,432,448,464,480,496,0,16,32,48,64,80,96,112,128,144,160,17..., dimensions={0} | all-to-all | bytes 131072 | tf_op jit(solution)/shard_map/all_to_all | solution.py:21
  26.5 0.5 shard_map.68
  27.0 0.0 copy-start
  27.0 15.2 %all_to_all.21 = bf16[16,16,1024]{2,1,0:T(8,128)(2,1)S(1)} all-to-all(bf16[16,16,1024]{2,1,0:T(8,128)(2,1)S(1)} %bitcast.8), channel_id=1, replica_groups={{9,10,11,12,13,14,15,0,1,2,3,4,5,6,7,8},{25,26,27,28,29,30,31,16,17,18,..., dimensions={0} | all-to-all | bytes 1048576 | tf_op jit(solution)/shard_map/all_to_all | solution.py:21
  42.2 0.0 copy-done
  42.2 1.7 %shard_map.69 = (bf16[256,1024]{1,0:T(8,128)(2,1)S(1)}, bf16[256,128]{1,0:T(8,128)(2,1)S(1)}, bf16[1024,256]{1,0:T(8,128)(2,1)}) custom-call(bf16[256,128]{1,0:T(8,128)(2,1)S(1)} %bitcast.10, bf16[256,1024]{1,0:T(8,128)(2,1)S(1)} %bitcast.6, bf16[1024,256]{1,0:T(8,128)(2,1)S(1)} %copy-done), custom_call_target="tpu_custom_call" | custom-call | tf_op jit(solution)/shard_map/pallas_call | solution.py:179
  43.9 12.6 %all_to_all.22 = bf16[16,16,1024]{2,1,0:T(8,128)(2,1)S(1)} all-to-all(bf16[16,16,1024]{2,1,0:T(8,128)(2,1)S(1)} %bitcast.11), channel_id=1, replica_groups={{9,10,11,12,13,14,15,0,1,2,3,4,5,6,7,8},{25,26,27,28,29,30,31,16,17,18,..., dimensions={0} | all-to-all | bytes 1048576 | tf_op jit(solution)/shard_map/all_to_all | solution.py:21
  56.5 0.7 shard_map.70
  57.2 17.5 %all_to_all.23 = bf16[32,4,2,128]{3,2,1,0:T(2,128)(2,1)S(1)} all-to-all(bf16[32,4,2,128]{3,2,1,0:T(2,128)(2,1)S(1)} %bitcast.12), channel_id=1, replica_groups={{384,400,416,432,448,464,480,496,0,16,32,48,64,80,96,112,128,144,160,17..., dimensions={0} | all-to-all | bytes 131072 | tf_op jit(solution)/shard_map/all_to_all | solution.py:21
  74.7 0.1 convert_reduce_fusion
  74.8 0.7 fusion
Async XLA Ops:
  27.0 15.2 %copy-start = (bf16[1024,256]{1,0:T(8,128)(2,1)S(1)}, bf16[1024,256]{1,0:T(8,128)(2,1)}, u32[]{:S(2)}) copy-start(bf16[1024,256]{1,0:T(8,128)(2,1)} %cotangent.1) | copy-start | bytes 1572868

commit v5 on v2

v5 whole, which is shorter than its diff:
```python
import functools

import jax
import jax.numpy as jnp
from jax import lax
from jax.experimental import pallas as pl
from jax.experimental.pallas import tpu as pltpu
from jax.sharding import PartitionSpec as P

NB = 64
BS = 64
F32, BF16 = jnp.float32, jnp.bfloat16
WEIGHTS_FIRST = 26
GRADS_FIRST = 24
MP_FIRST = 9
STEPS = (256, 512, 256)


def exchange(x, axis, first):
    size = lax.axis_size(axis)
    members = [(first + j) % size for j in range(size)]
    return lax.all_to_all(x, axis, 0, 0, axis_index_groups=[members], tiled=True)


def dot(a, b, ca, cb):
    return lax.dot_general(a, b, (((ca,), (cb,)), ((), ())), preferred_element_type=F32)


def div(x, n):
    return lax.shift_right_logical(x, jnp.int32(n.bit_length() - 1))


def mod(x, n):
    return x & (n - 1)


def one_hot(ref, of_row, of_column):
    rows, columns = ref.shape
    r = of_row(lax.broadcasted_iota(jnp.int32, (rows, 128), 0))
    c = of_column(lax.broadcasted_iota(jnp.int32, (1, columns), 1))
    same = jnp.concatenate([r] * (columns // 128), axis=1) == c
    ref[...] = jnp.where(same, 1.0, 0.0).astype(BF16)


class Plan:
    def __init__(self, groups, n_dp, held):
        self.groups, self.n_dp, self.held = groups, n_dp, held
        self.owned = NB // groups
        self.width = self.owned * BS
        self.line = self.owned * held
        assert all(n & (n - 1) == 0 for n in (groups, n_dp, held))

    def peer_m(self, r):
        return mod(div(r, self.held), self.owned)

    def peer_i(self, r):
        high = div(mod(r, self.owned * self.owned), self.line)
        return high * self.held + mod(r, self.held)

    def target(self, r):
        peer = mod(div(r, self.owned * self.owned) + MP_FIRST, self.groups)
        return peer * self.owned + self.peer_m(r)

    def feature(self, r, first):
        member = mod(div(r, self.line) + first, self.n_dp)
        return div(mod(r, self.line), self.held) * BS + member * self.held + mod(r, self.held)

    def turn(self, x, first, back):
        by = (MP_FIRST * self.owned * self.owned - first * self.line) % self.width
        by = self.width - by if back else by
        return jnp.concatenate([x[by:], x[:by]], axis=0) if by % self.width else x


def load_kernel(
    plan, right, left, tokens, copies, held, spread, unspread, tiles, wfeatures, gfeatures, block, m, r, l, sems
):
    rows = tokens.shape[0] // 4
    loads = [pltpu.make_async_copy(right, r, sems.at[0]), pltpu.make_async_copy(left, l, sems.at[1])]
    for k in range(4):
        at = pl.ds(k * rows, rows)
        loads.append(pltpu.make_async_copy(tokens.at[at, :], held.at[at, :], sems.at[2 + k]))
    for load in loads:
        load.start()
    one_hot(spread, plan.target, lambda c: c)
    one_hot(unspread, lambda n: n, plan.target)
    one_hot(tiles, lambda n: n, lambda c: mod(c, BS) + BS)
    one_hot(wfeatures, lambda n: plan.feature(n, WEIGHTS_FIRST), lambda c: c)
    one_hot(gfeatures, lambda n: plan.feature(n, GRADS_FIRST), lambda c: c)
    one_hot(block, plan.peer_i, lambda c: div(c, BS))
    one_hot(m, plan.peer_m, lambda c: div(c, BS))
    loads[0].wait()
    loads[1].wait()
    copies[...] = jnp.broadcast_to(jnp.concatenate([r[...], l[...]], axis=2), copies.shape)
    for load in loads[2:]:
        load.wait()


def first_kernel(plan, lines, tokens, spread, tiles, features, block, m, inner, left):
    right = dot(spread[...], lines[...], 1, 1).astype(BF16)
    right = dot(right, features[...], 1, 0).astype(BF16) * block[...]
    inner[...] = dot(right, tokens[...], 1, 1).astype(BF16)
    turned = plan.turn(lines[...], WEIGHTS_FIRST, False)
    left[...] = (dot(turned, tiles[...], 1, 0) * 0.5).astype(BF16) * m[...]


def middle_kernel(plan, left, inner, cotangent, tiles, m, dmixed, part_left, activated, act, pres, dpres, sems):
    steps, copies = len(STEPS), []
    spans = [pl.ds(sum(STEPS[:s]), STEPS[s]) for s in range(steps)]

    def pre_of(s):
        pres[spans[s], :] = dot(inner[:, spans[s]], left[...], 0, 0)

    def slope_of(s):
        at = spans[s]
        half = pres[at, :]
        twice_cdf = 1.0 + lax.erf(half * 1.4142135623730951)
        act[at, :] = (half * twice_cdf).astype(BF16)
        density = jnp.exp2(half * half * -2.8853900817779268) * 1.5957691216057308
        slope = twice_cdf + half * density
        dpres[at, :] = (cotangent[at, :].astype(F32) * slope).astype(BF16)

    def products_of(s, total):
        at = spans[s]
        dmixed[:, at] = dot(left[...], dpres[at, :], 1, 1).astype(BF16)
        part = dot(inner[:, at], dpres[at, :], 1, 0)
        return part if total is None else total + part

    total = None
    pre_of(0)
    for s in range(steps):
        if s + 1 < steps:
            pre_of(s + 1)
        slope_of(s)
        if s:
            total = products_of(s - 1, total)
        at = spans[s]
        copies.append(pltpu.make_async_copy(act.at[at, :], activated.at[at, :], sems.at[s]))
        copies[-1].start()
    total = products_of(steps - 1, total)
    part = (total * 0.5).astype(BF16) * m[...]
    part_left[...] = plan.turn(dot(part, tiles[...], 1, 1), GRADS_FIRST, True).astype(BF16)
    for copy in copies:
        copy.wait()


def last_kernel(plan, dinner, tokens, part_left, unspread, features, block, parts):
    part = dot(dinner[...], tokens[...], 1, 0).astype(BF16) * block[...]
    part = dot(unspread[...], part, 1, 0).astype(BF16)
    parts[...] = (dot(features[...], part, 1, 1) + part_left[...].astype(F32)).astype(BF16)


HBM = pl.BlockSpec(memory_space=pltpu.HBM)
VMEM = pl.BlockSpec(memory_space=pltpu.VMEM)


def call(kernel, inputs, outputs, scratch=(), hbm_in=False, hbm_out=(), limit=24):
    outs = tuple(
        jax.ShapeDtypeStruct(shape, BF16) if k in hbm_out else pltpu.VMEM(shape, BF16)
        for k, shape in enumerate(outputs)
    )
    return pl.pallas_call(
        kernel,
        out_shape=outs,
        in_specs=[HBM if hbm_in else VMEM] * len(inputs),
        out_specs=tuple(HBM if k in hbm_out else VMEM for k in range(len(outs))),
        scratch_shapes=scratch,
        compiler_params=pltpu.CompilerParams(vmem_limit_bytes=limit * 1024 * 1024),
    )(*inputs)


def shards(tokens, right_weight, left_weight, cotangent):
    rows = tokens.shape[0]
    groups, n_dp = lax.axis_size("mp"), lax.axis_size("dp")
    plan = Plan(groups, n_dp, right_weight.shape[1])
    width = plan.width
    line = (*right_weight.shape[:2], 2 * BS)
    square, tall, wide = (width, width), (width, 2 * BS), (2 * BS, width)

    copies, tokens, spread, unspread, tiles, wfeatures, gfeatures, block, m = call(
        functools.partial(load_kernel, plan),
        (right_weight, left_weight, tokens),
        ((n_dp, *line), tokens.shape, tall, wide, wide, square, square, square, square),
        scratch=[
            pltpu.VMEM(right_weight.shape, BF16),
            pltpu.VMEM(left_weight.shape, BF16),
            pltpu.SemaphoreType.DMA((6,)),
        ],
        hbm_in=True,
        limit=60,
    )
    lines = exchange(copies, "dp", WEIGHTS_FIRST).reshape(tall)

    inner, left = call(
        functools.partial(first_kernel, plan),
        (lines, tokens, spread, tiles, wfeatures, block, m),
        ((width, rows), square),
    )
    inner = exchange(inner.reshape(groups, -1, rows), "mp", MP_FIRST).reshape(width, rows)

    dmixed, part_left, activated = call(
        functools.partial(middle_kernel, plan),
        (left, inner, cotangent, tiles, m),
        ((width, rows), tall, (rows, width)),
        scratch=[
            pltpu.VMEM((rows, width), BF16),
            pltpu.VMEM((rows, width), F32),
            pltpu.VMEM((rows, width), BF16),
            pltpu.SemaphoreType.DMA((len(STEPS),)),
        ],
        hbm_out=(2,),
    )
    dinner = exchange(dmixed.reshape(groups, -1, rows), "mp", MP_FIRST).reshape(width, rows)

    (parts,) = call(
        functools.partial(last_kernel, plan),
        (dinner, tokens, part_left, unspread, gfeatures, block),
        (tall,),
    )
    sums = jnp.sum(exchange(parts.reshape(n_dp, *line), "dp", GRADS_FIRST).astype(F32), axis=0)
    return (activated, sums[..., :BS], sums[..., BS:])


def solution(mesh):
    return jax.shard_map(
        shards,
        mesh=mesh,
        in_specs=(P("dp", "mp"), P("mp", "dp", None), P("mp", "dp", None), P("dp", "mp")),
        out_specs=(P("dp", "mp"), P("mp", "dp", None), P("mp", "dp", None)),
        check_vma=False,
    )
```

time: 81.8 us -> 75.8 us (0.927)
  blocking collectives: 0 us -> 70 us
  starting transfers between devices: 49.9 us -> 0 us
  waiting for transfers between devices: 20.5 us -> 0 us
  matrix products: 4.06 us -> 0 us
  local copies, waits for them, and re-layouts: 4.66 us -> 0.68 us
  Pallas kernels: 0 us -> 3.84 us
  other arithmetic: 1.48 us -> 0.07 us
    all_to_all x0 -> x4, blocking collectives: none -> 70 us  [exchange(): lax.all_to_all(x, axis, 0, 0, axis_index_groups=[members], tiled=True)]
    all_to_all x4 -> x0, starting transfers between devices: 49.9 us -> none  [exchange(): lax.all_to_all(x, axis, 0, 0, axis_index_groups=[members], tiled=True)]
    all_to_all x4 -> x0, waiting for transfers between devices: 20.5 us -> none  [exchange(): lax.all_to_all(x, axis, 0, 0, axis_index_groups=[members], tiled=True)]
    dot_general x5 -> x0, matrix products: 4.06 us -> none  [dot(): lax.dot_general(a, b, (((ca,), (cb,)), ((), ())), preferred_element_type=...]
    pallas_call x0 -> x4, Pallas kernels: none -> 3.84 us  [call(): pl.pallas_call(kernel, out_shape=outs, in_specs=[HBM if hbm_in else VMEM]...]
    unnamed x10 -> x2, local copies, waits for them, and re-layouts: 1.89 us -> 0.01 us
    concatenate x4 -> x0, other arithmetic: 1.07 us -> none  [the longest x1 0.83 us: shards(): mine = jnp.concatenate([right_weight, left_weight], axis=2)]
  transfers between devices with their start and end apart: 4 -> 0, of which waited for: 4 -> 0; matrix products, arithmetic and copies ran while one was open for 3% -> 0% of each run, Pallas kernels for 0% -> 0%
where the time goes in v5:
time: 75.8 us; the launch traced here: 75.3 us
  blocking collectives  70 us (92%)
  Pallas kernels  3.84 us (5%)
    all_to_all x4, blocking collectives, exchange(): lax.all_to_all(x, axis, 0, 0, axis_index_groups=[members], tiled=True)  70 us
    pallas_call x4, Pallas kernels, call(): pl.pallas_call(kernel, out_shape=outs, in_specs=[HBM if hbm_in else VMEM]...  3.84 us

profile of v5, /device:TPU:1, one launch (start us, length us, event | category | flops | bytes accessed | tf_op | source)
XLA Modules:
  0.0 75.3 jit_solution(11436780838812487397)
XLA Ops:
  0.6 1.2 %shard_map.67 = (bf16[32,4,2,128]{3,2,1,0:T(2,128)(2,1)S(1)}, bf16[1024,256]{1,0:T(8,128)(2,1)S(1)}, bf16[256,128]{1,0:T(8,128)(2,1)S(1)}, bf16[128,256]{1,0:T(8...) custom-call(bf16[4,2,64]{2,1,0:T(2,128)(2,1)} %right.1, ...), custom_call_target="tpu_custom_call" | custom-call | tf_op jit(solution)/shard_map/pallas_call | solution.py:161
  1.8 24.6 %all_to_all.20 = bf16[32,4,2,128]{3,2,1,0:T(2,128)(2,1)S(1)} all-to-all(bf16[32,4,2,128]{3,2,1,0:T(2,128)(2,1)S(1)} %get-tuple-element.17), channel_id=1, replica_groups={{416,432,448,464,480,496,0,16,32,48,64,80,96,112,128,144,160,176,192,20..., dimensions={0} | all-to-all | bytes 131072 | tf_op jit(solution)/shard_map/all_to_all | solution.py:22
  26.4 0.6 shard_map.68
  27.0 0.0 copy-start
  27.0 15.3 %all_to_all.21 = bf16[16,16,1024]{2,1,0:T(8,128)(2,1)S(1)} all-to-all(bf16[16,16,1024]{2,1,0:T(8,128)(2,1)S(1)} %bitcast.9), channel_id=1, replica_groups={{9,10,11,12,13,14,15,0,1,2,3,4,5,6,7,8},{25,26,27,28,29,30,31,16,17,18,..., dimensions={0} | all-to-all | bytes 1048576 | tf_op jit(solution)/shard_map/all_to_all | solution.py:22
  42.3 0.0 copy-done
  42.3 1.4 %shard_map.69 = (bf16[256,1024]{1,0:T(8,128)(2,1)S(1)}, bf16[256,128]{1,0:T(8,128)(2,1)S(1)}, bf16[1024,256]{1,0:T(8,128)(2,1)}) custom-call(bf16[256,256]{1,0:T(8,128)(2,1)S(1)} %get-tuple-element.24.left, bf16[256,1024]{1,0:T(8,128)(2,1)S(1)} %bitcast.7, bf16[1024,256]{1,0:T(8,128)(2,1)S(1)} %copy-done, bf16[128,256]{1,0:T(8,128)(2,1)S(1)} %get-tuple-element.20.tiles, ...), custom_call_target="tpu_custom_call" | custom-call | tf_op jit(solution)/shard_map/pallas_call | solution.py:161
  43.7 12.6 %all_to_all.22 = bf16[16,16,1024]{2,1,0:T(8,128)(2,1)S(1)} all-to-all(bf16[16,16,1024]{2,1,0:T(8,128)(2,1)S(1)} %bitcast.8), channel_id=1, replica_groups={{9,10,11,12,13,14,15,0,1,2,3,4,5,6,7,8},{25,26,27,28,29,30,31,16,17,18,..., dimensions={0} | all-to-all | bytes 1048576 | tf_op jit(solution)/shard_map/all_to_all | solution.py:22
  56.3 0.7 shard_map.70
  57.0 17.5 %all_to_all.23 = bf16[32,4,2,128]{3,2,1,0:T(2,128)(2,1)S(1)} all-to-all(bf16[32,4,2,128]{3,2,1,0:T(2,128)(2,1)S(1)} %bitcast.10), channel_id=1, replica_groups={{384,400,416,432,448,464,480,496,0,16,32,48,64,80,96,112,128,144,160,17..., dimensions={0} | all-to-all | bytes 131072 | tf_op jit(solution)/shard_map/all_to_all | solution.py:22
  74.5 0.1 convert_reduce_fusion
  74.6 0.7 fusion
Async XLA Ops:
  27.0 15.3 %copy-start = (bf16[1024,256]{1,0:T(8,128)(2,1)S(1)}, bf16[1024,256]{1,0:T(8,128)(2,1)}, u32[]{:S(2)}) copy-start(bf16[1024,256]{1,0:T(8,128)(2,1)} %cotangent.1) | copy-start | bytes 1572868

commit v6 on v5

--- a/solution.py
+++ b/solution.py
@@ -71,14 +71,8 @@
         return jnp.concatenate([x[by:], x[:by]], axis=0) if by % self.width else x
 
 
-def load_kernel(
-    plan, right, left, tokens, copies, held, spread, unspread, tiles, wfeatures, gfeatures, block, m, r, l, sems
-):
-    rows = tokens.shape[0] // 4
+def load_kernel(plan, right, left, copies, spread, unspread, tiles, wfeatures, gfeatures, block, m, r, l, sems):
     loads = [pltpu.make_async_copy(right, r, sems.at[0]), pltpu.make_async_copy(left, l, sems.at[1])]
-    for k in range(4):
-        at = pl.ds(k * rows, rows)
-        loads.append(pltpu.make_async_copy(tokens.at[at, :], held.at[at, :], sems.at[2 + k]))
     for load in loads:
         load.start()
     one_hot(spread, plan.target, lambda c: c)
@@ -88,17 +82,14 @@
     one_hot(gfeatures, lambda n: plan.feature(n, GRADS_FIRST), lambda c: c)
     one_hot(block, plan.peer_i, lambda c: div(c, BS))
     one_hot(m, plan.peer_m, lambda c: div(c, BS))
-    loads[0].wait()
-    loads[1].wait()
+    for load in loads:
+        load.wait()
     copies[...] = jnp.broadcast_to(jnp.concatenate([r[...], l[...]], axis=2), copies.shape)
-    for load in loads[2:]:
-        load.wait()
-
-
-def first_kernel(plan, lines, tokens, spread, tiles, features, block, m, inner, left):
-    right = dot(spread[...], lines[...], 1, 1).astype(BF16)
-    right = dot(right, features[...], 1, 0).astype(BF16) * block[...]
-    inner[...] = dot(right, tokens[...], 1, 1).astype(BF16)
+
+
+def first_kernel(plan, lines, spread, tiles, features, block, m, right, left):
+    some = dot(spread[...], lines[...], 1, 1).astype(BF16)
+    right[...] = dot(some, features[...], 1, 0).astype(BF16) * block[...]
     turned = plan.turn(lines[...], WEIGHTS_FIRST, False)
     left[...] = (dot(turned, tiles[...], 1, 0) * 0.5).astype(BF16) * m[...]
 
@@ -143,9 +134,8 @@
         copy.wait()
 
 
-def last_kernel(plan, dinner, tokens, part_left, unspread, features, block, parts):
-    part = dot(dinner[...], tokens[...], 1, 0).astype(BF16) * block[...]
-    part = dot(unspread[...], part, 1, 0).astype(BF16)
+def last_kernel(plan, part, part_left, unspread, features, parts):
+    part = dot(unspread[...], part[...], 1, 0).astype(BF16)
     parts[...] = (dot(features[...], part, 1, 1) + part_left[...].astype(F32)).astype(BF16)
 
 
@@ -176,25 +166,26 @@
     line = (*right_weight.shape[:2], 2 * BS)
     square, tall, wide = (width, width), (width, 2 * BS), (2 * BS, width)
 
-    copies, tokens, spread, unspread, tiles, wfeatures, gfeatures, block, m = call(
+    copies, spread, unspread, tiles, wfeatures, gfeatures, block, m = call(
         functools.partial(load_kernel, plan),
-        (right_weight, left_weight, tokens),
-        ((n_dp, *line), tokens.shape, tall, wide, wide, square, square, square, square),
+        (right_weight, left_weight),
+        ((n_dp, *line), tall, wide, wide, square, square, square, square),
         scratch=[
             pltpu.VMEM(right_weight.shape, BF16),
             pltpu.VMEM(left_weight.shape, BF16),
-            pltpu.SemaphoreType.DMA((6,)),
+            pltpu.SemaphoreType.DMA((2,)),
         ],
         hbm_in=True,
         limit=60,
     )
     lines = exchange(copies, "dp", WEIGHTS_FIRST).reshape(tall)
 
-    inner, left = call(
+    right, left = call(
         functools.partial(first_kernel, plan),
-        (lines, tokens, spread, tiles, wfeatures, block, m),
-        ((width, rows), square),
-    )
+        (lines, spread, tiles, wfeatures, block, m),
+        (square, square),
+    )
+    inner = dot(right, tokens, 1, 1).astype(BF16)
     inner = exchange(inner.reshape(groups, -1, rows), "mp", MP_FIRST).reshape(width, rows)
 
     dmixed, part_left, activated = call(
@@ -211,9 +202,10 @@
     )
     dinner = exchange(dmixed.reshape(groups, -1, rows), "mp", MP_FIRST).reshape(width, rows)
 
+    part = dot(dinner, tokens, 1, 0).astype(BF16) * block
     (parts,) = call(
         functools.partial(last_kernel, plan),
-        (dinner, tokens, part_left, unspread, gfeatures, block),
+        (part, part_left, unspread, gfeatures),
         (tall,),
     )
     sums = jnp.sum(exchange(parts.reshape(n_dp, *line), "dp", GRADS_FIRST).astype(F32), axis=0)

time: 75.8 us -> 75.6 us (level)
  Pallas kernels: 3.84 us -> 2.97 us
    pallas_call x4, Pallas kernels: 3.84 us -> 2.97 us  [call(): pl.pallas_call(kernel, out_shape=outs, in_specs=[HBM if hbm_in else VMEM]...]
where the time goes in v6:
time: 75.6 us; the launch traced here: 75.1 us
  blocking collectives  70 us (93%)
  Pallas kernels  2.97 us (4%)
    all_to_all x4, blocking collectives, exchange(): lax.all_to_all(x, axis, 0, 0, axis_index_groups=[members], tiled=True)  70 us
    pallas_call x4, Pallas kernels, call(): pl.pallas_call(kernel, out_shape=outs, in_specs=[HBM if hbm_in else VMEM]...  2.97 us

profile of v6, /device:TPU:1, one launch (start us, length us, event | category | flops | bytes accessed | tf_op | source)
XLA Modules:
  0.0 75.1 jit_solution(11945289861385322954)
XLA Ops:
  0.6 0.0 copy-start
  0.6 0.9 %shard_map.67 = (bf16[32,4,2,128]{3,2,1,0:T(2,128)(2,1)S(1)}, bf16[256,128]{1,0:T(8,128)(2,1)S(1)}, bf16[128,256]{1,0:T(8,128)(2,1)S(1)}, bf16[128,256]{1,0:T(8,...) custom-call(bf16[4,2,64]{2,1,0:T(2,128)(2,1)} %right.1, ...), custom_call_target="tpu_custom_call" | custom-call | tf_op jit(solution)/shard_map/pallas_call | solution.py:151
  1.5 24.6 %all_to_all.20 = bf16[32,4,2,128]{3,2,1,0:T(2,128)(2,1)S(1)} all-to-all(bf16[32,4,2,128]{3,2,1,0:T(2,128)(2,1)S(1)} %get-tuple-element.16), channel_id=1, replica_groups={{416,432,448,464,480,496,0,16,32,48,64,80,96,112,128,144,160,176,192,20..., dimensions={0} | all-to-all | bytes 131072 | tf_op jit(solution)/shard_map/all_to_all | solution.py:22
  26.2 0.3 shard_map.68
  26.5 0.0 copy-done
  26.5 0.3 convolution_convert_fusion
  26.9 0.0 copy-start.1
  26.9 15.3 %all_to_all.21 = bf16[16,16,1024]{2,1,0:T(8,128)(2,1)S(1)} all-to-all(bf16[16,16,1024]{2,1,0:T(8,128)(2,1)S(1)} %bitcast.15), channel_id=1, replica_groups={{9,10,11,12,13,14,15,0,1,2,3,4,5,6,7,8},{25,26,27,28,29,30,31,16,17,18,..., dimensions={0} | all-to-all | bytes 1048576 | tf_op jit(solution)/shard_map/all_to_all | solution.py:22
  42.1 0.0 copy-done.1
  42.1 1.4 %shard_map.69 = (bf16[256,1024]{1,0:T(8,128)(2,1)S(1)}, bf16[256,128]{1,0:T(8,128)(2,1)S(1)}, bf16[1024,256]{1,0:T(8,128)(2,1)}) custom-call(bf16[256,256]{1,0:T(8,128)(2,1)S(1)} %get-tuple-element.22.left, bf16[256,1024]{1,0:T(8,128)(2,1)S(1)} %bitcast.10, bf16[1024,256]{1,0:T(8,128)(2,1)S(1)} %copy-done.1, bf16[128,256]{1,0:T(8,128)(2,1)S(1)} %get-tuple-element.18.tiles, ...), custom_call_target="tpu_custom_call" | custom-call | tf_op jit(solution)/shard_map/pallas_call | solution.py:151
  43.5 12.6 %all_to_all.22 = bf16[16,16,1024]{2,1,0:T(8,128)(2,1)S(1)} all-to-all(bf16[16,16,1024]{2,1,0:T(8,128)(2,1)S(1)} %bitcast.11), channel_id=1, replica_groups={{9,10,11,12,13,14,15,0,1,2,3,4,5,6,7,8},{25,26,27,28,29,30,31,16,17,18,..., dimensions={0} | all-to-all | bytes 1048576 | tf_op jit(solution)/shard_map/all_to_all | solution.py:22
  56.1 0.3 fusion.part
  56.4 0.4 shard_map.70
  56.8 17.5 %all_to_all.23 = bf16[32,4,2,128]{3,2,1,0:T(2,128)(2,1)S(1)} all-to-all(bf16[32,4,2,128]{3,2,1,0:T(2,128)(2,1)S(1)} %bitcast.13), channel_id=1, replica_groups={{384,400,416,432,448,464,480,496,0,16,32,48,64,80,96,112,128,144,160,17..., dimensions={0} | all-to-all | bytes 131072 | tf_op jit(solution)/shard_map/all_to_all | solution.py:22
  74.3 0.1 convert_reduce_fusion
  74.4 0.7 fusion.1
Async XLA Ops:
  0.6 25.9 %copy-start = (bf16[1024,256]{1,0:T(8,128)(2,1)S(1)}, bf16[1024,256]{1,0:T(8,128)(2,1)}, u32[]{:S(2)}) copy-start(bf16[1024,256]{1,0:T(8,128)(2,1)} %param.4) | copy-start | bytes 1572868
  26.9 15.3 %copy-start.1 = (bf16[1024,256]{1,0:T(8,128)(2,1)S(1)}, bf16[1024,256]{1,0:T(8,128)(2,1)}, u32[]{:S(2)}) copy-start(bf16[1024,256]{1,0:T(8,128)(2,1)} %cotangent.1) | copy-start | bytes 1572868

commit v7 on v6

--- a/solution.py
+++ b/solution.py
@@ -10,8 +10,7 @@
 NB = 64
 BS = 64
 F32, BF16 = jnp.float32, jnp.bfloat16
-WEIGHTS_FIRST = 26
-GRADS_FIRST = 24
+DP_FIRST = 24
 MP_FIRST = 9
 STEPS = (256, 512, 256)
 
@@ -71,15 +70,14 @@
         return jnp.concatenate([x[by:], x[:by]], axis=0) if by % self.width else x
 
 
-def load_kernel(plan, right, left, copies, spread, unspread, tiles, wfeatures, gfeatures, block, m, r, l, sems):
+def load_kernel(plan, right, left, copies, spread, unspread, tiles, features, block, m, r, l, sems):
     loads = [pltpu.make_async_copy(right, r, sems.at[0]), pltpu.make_async_copy(left, l, sems.at[1])]
     for load in loads:
         load.start()
     one_hot(spread, plan.target, lambda c: c)
     one_hot(unspread, lambda n: n, plan.target)
     one_hot(tiles, lambda n: n, lambda c: mod(c, BS) + BS)
-    one_hot(wfeatures, lambda n: plan.feature(n, WEIGHTS_FIRST), lambda c: c)
-    one_hot(gfeatures, lambda n: plan.feature(n, GRADS_FIRST), lambda c: c)
+    one_hot(features, lambda n: plan.feature(n, DP_FIRST), lambda c: c)
     one_hot(block, plan.peer_i, lambda c: div(c, BS))
     one_hot(m, plan.peer_m, lambda c: div(c, BS))
     for load in loads:
@@ -90,7 +88,7 @@
 def first_kernel(plan, lines, spread, tiles, features, block, m, right, left):
     some = dot(spread[...], lines[...], 1, 1).astype(BF16)
     right[...] = dot(some, features[...], 1, 0).astype(BF16) * block[...]
-    turned = plan.turn(lines[...], WEIGHTS_FIRST, False)
+    turned = plan.turn(lines[...], DP_FIRST, False)
     left[...] = (dot(turned, tiles[...], 1, 0) * 0.5).astype(BF16) * m[...]
 
 
@@ -129,7 +127,7 @@
         copies[-1].start()
     total = products_of(steps - 1, total)
     part = (total * 0.5).astype(BF16) * m[...]
-    part_left[...] = plan.turn(dot(part, tiles[...], 1, 1), GRADS_FIRST, True).astype(BF16)
+    part_left[...] = plan.turn(dot(part, tiles[...], 1, 1), DP_FIRST, True).astype(BF16)
     for copy in copies:
         copy.wait()
 
@@ -166,10 +164,10 @@
     line = (*right_weight.shape[:2], 2 * BS)
     square, tall, wide = (width, width), (width, 2 * BS), (2 * BS, width)
 
-    copies, spread, unspread, tiles, wfeatures, gfeatures, block, m = call(
+    copies, spread, unspread, tiles, features, block, m = call(
         functools.partial(load_kernel, plan),
         (right_weight, left_weight),
-        ((n_dp, *line), tall, wide, wide, square, square, square, square),
+        ((n_dp, *line), tall, wide, wide, square, square, square),
         scratch=[
             pltpu.VMEM(right_weight.shape, BF16),
             pltpu.VMEM(left_weight.shape, BF16),
@@ -178,11 +176,11 @@
         hbm_in=True,
         limit=60,
     )
-    lines = exchange(copies, "dp", WEIGHTS_FIRST).reshape(tall)
+    lines = exchange(copies, "dp", DP_FIRST).reshape(tall)
 
     right, left = call(
         functools.partial(first_kernel, plan),
-        (lines, spread, tiles, wfeatures, block, m),
+        (lines, spread, tiles, features, block, m),
         (square, square),
     )
     inner = dot(right, tokens, 1, 1).astype(BF16)
@@ -205,11 +203,13 @@
     part = dot(dinner, tokens, 1, 0).astype(BF16) * block
     (parts,) = call(
         functools.partial(last_kernel, plan),
-        (part, part_left, unspread, gfeatures),
+        (part, part_left, unspread, features),
         (tall,),
     )
-    sums = jnp.sum(exchange(parts.reshape(n_dp, *line), "dp", GRADS_FIRST).astype(F32), axis=0)
-    return (activated, sums[..., :BS], sums[..., BS:])
+    parts = exchange(parts.reshape(n_dp, *line), "dp", DP_FIRST)
+    right = jnp.sum(parts[..., :BS].astype(F32), axis=0)
+    left = jnp.sum(parts[..., BS:].astype(F32), axis=0)
+    return (activated, right, left)
 
 
 def solution(mesh):

time: 75.6 us -> 75.7 us (level)
  no operation moved by 1% of the time
where the time goes in v7:
time: 75.7 us; the launch traced here: 75.1 us
  blocking collectives  70 us (92%)
  Pallas kernels  2.97 us (4%)
  other arithmetic  0.8 us (1%)
    all_to_all x4, blocking collectives, exchange(): lax.all_to_all(x, axis, 0, 0, axis_index_groups=[members], tiled=True)  70 us
    pallas_call x4, Pallas kernels, call(): pl.pallas_call(kernel, out_shape=outs, in_specs=[HBM if hbm_in else VMEM]...  2.97 us

profile of v7, /device:TPU:1, one launch (start us, length us, event | category | flops | bytes accessed | tf_op | source)
XLA Modules:
  0.0 75.1 jit_solution(10802608079853592854)
XLA Ops:
  0.6 0.0 copy-start
  0.6 0.9 %shard_map.67 = (bf16[32,4,2,128]{3,2,1,0:T(2,128)(2,1)S(1)}, bf16[256,128]{1,0:T(8,128)(2,1)S(1)}, bf16[128,256]{1,0:T(8,128)(2,1)S(1)}, bf16[128,256]{1,0:T(8,...) custom-call(bf16[4,2,64]{2,1,0:T(2,128)(2,1)} %right.1, ...), custom_call_target="tpu_custom_call" | custom-call | tf_op jit(solution)/shard_map/pallas_call | solution.py:149
  1.5 24.7 %all_to_all.20 = bf16[32,4,2,128]{3,2,1,0:T(2,128)(2,1)S(1)} all-to-all(bf16[32,4,2,128]{3,2,1,0:T(2,128)(2,1)S(1)} %get-tuple-element.15), channel_id=1, replica_groups={{384,400,416,432,448,464,480,496,0,16,32,48,64,80,96,112,128,144,160,17..., dimensions={0} | all-to-all | bytes 131072 | tf_op jit(solution)/shard_map/all_to_all | solution.py:21
  26.3 0.3 shard_map.68
  26.6 0.0 copy-done
  26.6 0.3 convolution_convert_fusion
  27.0 0.0 copy-start.1
  27.0 15.2 %all_to_all.21 = bf16[16,16,1024]{2,1,0:T(8,128)(2,1)S(1)} all-to-all(bf16[16,16,1024]{2,1,0:T(8,128)(2,1)S(1)} %bitcast.15), channel_id=1, replica_groups={{9,10,11,12,13,14,15,0,1,2,3,4,5,6,7,8},{25,26,27,28,29,30,31,16,17,18,..., dimensions={0} | all-to-all | bytes 1048576 | tf_op jit(solution)/shard_map/all_to_all | solution.py:21
  42.2 0.0 copy-done.1
  42.2 1.4 %shard_map.69 = (bf16[256,1024]{1,0:T(8,128)(2,1)S(1)}, bf16[256,128]{1,0:T(8,128)(2,1)S(1)}, bf16[1024,256]{1,0:T(8,128)(2,1)}) custom-call(bf16[256,256]{1,0:T(8,128)(2,1)S(1)} %get-tuple-element.21.left, bf16[256,1024]{1,0:T(8,128)(2,1)S(1)} %bitcast.10, bf16[1024,256]{1,0:T(8,128)(2,1)S(1)} %copy-done.1, bf16[128,256]{1,0:T(8,128)(2,1)S(1)} %get-tuple-element.17.tiles, ...), custom_call_target="tpu_custom_call" | custom-call | tf_op jit(solution)/shard_map/pallas_call | solution.py:149
  43.6 12.6 %all_to_all.22 = bf16[16,16,1024]{2,1,0:T(8,128)(2,1)S(1)} all-to-all(bf16[16,16,1024]{2,1,0:T(8,128)(2,1)S(1)} %bitcast.11), channel_id=1, replica_groups={{9,10,11,12,13,14,15,0,1,2,3,4,5,6,7,8},{25,26,27,28,29,30,31,16,17,18,..., dimensions={0} | all-to-all | bytes 1048576 | tf_op jit(solution)/shard_map/all_to_all | solution.py:21
  56.2 0.3 fusion.part
  56.5 0.4 shard_map.70
  56.8 17.5 %all_to_all.23 = bf16[32,4,2,128]{3,2,1,0:T(2,128)(2,1)S(1)} all-to-all(bf16[32,4,2,128]{3,2,1,0:T(2,128)(2,1)S(1)} %bitcast.13), channel_id=1, replica_groups={{384,400,416,432,448,464,480,496,0,16,32,48,64,80,96,112,128,144,160,17..., dimensions={0} | all-to-all | bytes 131072 | tf_op jit(solution)/shard_map/all_to_all | solution.py:21
  74.3 0.8 %convert_reduce_fusion = (f32[4,2,64]{2,1,0:T(2,128)}, f32[4,2,64]{2,1,0:T(2,128)}) fusion(bf16[32,4,2,128]{3,2,1,0:T(2,128)(2,1)S(1)} %all_to_all.23), kind=kLoop, calls=%fused_computation.3 | loop fusion | flops 64512 | bytes 69632 | tf_op jit(solution)/shard_map/reduce_sum | solution.py:211
Async XLA Ops:
  0.6 26.0 %copy-start = (bf16[1024,256]{1,0:T(8,128)(2,1)S(1)}, bf16[1024,256]{1,0:T(8,128)(2,1)}, u32[]{:S(2)}) copy-start(bf16[1024,256]{1,0:T(8,128)(2,1)} %param.4) | copy-start | bytes 1572868
  27.0 15.2 %copy-start.1 = (bf16[1024,256]{1,0:T(8,128)(2,1)S(1)}, bf16[1024,256]{1,0:T(8,128)(2,1)}, u32[]{:S(2)}) copy-start(bf16[1024,256]{1,0:T(8,128)(2,1)} %cotangent.1) | copy-start | bytes 1572868

commit v8 on v7

--- a/solution.py
+++ b/solution.py
@@ -132,11 +132,6 @@
         copy.wait()
 
 
-def last_kernel(plan, part, part_left, unspread, features, parts):
-    part = dot(unspread[...], part[...], 1, 0).astype(BF16)
-    parts[...] = (dot(features[...], part, 1, 1) + part_left[...].astype(F32)).astype(BF16)
-
-
 HBM = pl.BlockSpec(memory_space=pltpu.HBM)
 VMEM = pl.BlockSpec(memory_space=pltpu.VMEM)
 
@@ -201,11 +196,8 @@
     dinner = exchange(dmixed.reshape(groups, -1, rows), "mp", MP_FIRST).reshape(width, rows)
 
     part = dot(dinner, tokens, 1, 0).astype(BF16) * block
-    (parts,) = call(
-        functools.partial(last_kernel, plan),
-        (part, part_left, unspread, features),
-        (tall,),
-    )
+    part = dot(unspread, part, 1, 0).astype(BF16)
+    parts = (dot(features, part, 1, 1) + part_left.astype(F32)).astype(BF16)
     parts = exchange(parts.reshape(n_dp, *line), "dp", DP_FIRST)
     right = jnp.sum(parts[..., :BS].astype(F32), axis=0)
     left = jnp.sum(parts[..., BS:].astype(F32), axis=0)

time: 75.7 us -> 75.7 us (level)
    pallas_call x4 -> x3, Pallas kernels: 2.97 us -> 2.61 us  [call(): pl.pallas_call(kernel, out_shape=outs, in_specs=[HBM if hbm_in else VMEM]...]
where the time goes in v8:
time: 75.7 us; the launch traced here: 75.2 us
  blocking collectives  70 us (92%)
  Pallas kernels  2.61 us (3%)
  matrix products  1.01 us (1%)
  other arithmetic  0.8 us (1%)
    all_to_all x4, blocking collectives, exchange(): lax.all_to_all(x, axis, 0, 0, axis_index_groups=[members], tiled=True)  70 us
    pallas_call x3, Pallas kernels, call(): pl.pallas_call(kernel, out_shape=outs, in_specs=[HBM if hbm_in else VMEM]...  2.61 us

profile of v8, /device:TPU:1, one launch (start us, length us, event | category | flops | bytes accessed | tf_op | source)
XLA Modules:
  0.0 75.2 jit_solution(10114903362366882551)
XLA Ops:
  0.6 0.0 copy-start
  0.6 0.9 %shard_map.67 = (bf16[32,4,2,128]{3,2,1,0:T(2,128)(2,1)S(1)}, bf16[256,128]{1,0:T(8,128)(2,1)S(1)}, bf16[128,256]{1,0:T(8,128)(2,1)S(1)}, bf16[128,256]{1,0:T(8,...) custom-call(bf16[4,2,64]{2,1,0:T(2,128)(2,1)} %right.1, ...), custom_call_target="tpu_custom_call" | custom-call | tf_op jit(solution)/shard_map/pallas_call | solution.py:144
  1.5 24.7 %all_to_all.20 = bf16[32,4,2,128]{3,2,1,0:T(2,128)(2,1)S(1)} all-to-all(bf16[32,4,2,128]{3,2,1,0:T(2,128)(2,1)S(1)} %get-tuple-element.15), channel_id=1, replica_groups={{384,400,416,432,448,464,480,496,0,16,32,48,64,80,96,112,128,144,160,17..., dimensions={0} | all-to-all | bytes 131072 | tf_op jit(solution)/shard_map/all_to_all | solution.py:21
  26.3 0.3 shard_map.68
  26.6 0.0 copy-done
  26.6 0.3 convolution_convert_fusion
  27.0 0.0 copy-start.1
  27.0 15.2 %all_to_all.21 = bf16[16,16,1024]{2,1,0:T(8,128)(2,1)S(1)} all-to-all(bf16[16,16,1024]{2,1,0:T(8,128)(2,1)S(1)} %bitcast.17), channel_id=1, replica_groups={{9,10,11,12,13,14,15,0,1,2,3,4,5,6,7,8},{25,26,27,28,29,30,31,16,17,18,..., dimensions={0} | all-to-all | bytes 1048576 | tf_op jit(solution)/shard_map/all_to_all | solution.py:21
  42.2 0.0 copy-done.1
  42.2 1.4 %shard_map.69 = (bf16[256,1024]{1,0:T(8,128)(2,1)S(1)}, bf16[256,128]{1,0:T(8,128)(2,1)S(1)}, bf16[1024,256]{1,0:T(8,128)(2,1)}) custom-call(bf16[256,256]{1,0:T(8,128)(2,1)S(1)} %get-tuple-element.21.left, bf16[256,1024]{1,0:T(8,128)(2,1)S(1)} %bitcast.13, bf16[1024,256]{1,0:T(8,128)(2,1)S(1)} %copy-done.1, bf16[128,256]{1,0:T(8,128)(2,1)S(1)} %get-tuple-element.17.tiles, ...), custom_call_target="tpu_custom_call" | custom-call | tf_op jit(solution)/shard_map/pallas_call | solution.py:144
  43.6 12.6 %all_to_all.22 = bf16[16,16,1024]{2,1,0:T(8,128)(2,1)S(1)} all-to-all(bf16[16,16,1024]{2,1,0:T(8,128)(2,1)S(1)} %bitcast.14), channel_id=1, replica_groups={{9,10,11,12,13,14,15,0,1,2,3,4,5,6,7,8},{25,26,27,28,29,30,31,16,17,18,..., dimensions={0} | all-to-all | bytes 1048576 | tf_op jit(solution)/shard_map/all_to_all | solution.py:21
  56.2 0.5 fusion.2
  56.7 0.2 fusion.3
  56.9 17.5 %all_to_all.23 = bf16[32,4,2,128]{3,2,1,0:T(2,128)(2,1)S(1)} all-to-all(bf16[32,4,2,128]{3,2,1,0:T(2,128)(2,1)S(1)} %bitcast.18), channel_id=1, replica_groups={{384,400,416,432,448,464,480,496,0,16,32,48,64,80,96,112,128,144,160,17..., dimensions={0} | all-to-all | bytes 131072 | tf_op jit(solution)/shard_map/all_to_all | solution.py:21
  74.4 0.8 %convert_reduce_fusion = (f32[4,2,64]{2,1,0:T(2,128)}, f32[4,2,64]{2,1,0:T(2,128)}) fusion(bf16[32,4,2,128]{3,2,1,0:T(2,128)(2,1)S(1)} %all_to_all.23), kind=kLoop, calls=%fused_computation.7 | loop fusion | flops 64512 | bytes 69632 | tf_op jit(solution)/shard_map/reduce_sum | solution.py:203
Async XLA Ops:
  0.6 26.0 %copy-start = (bf16[1024,256]{1,0:T(8,128)(2,1)S(1)}, bf16[1024,256]{1,0:T(8,128)(2,1)}, u32[]{:S(2)}) copy-start(bf16[1024,256]{1,0:T(8,128)(2,1)} %param.4) | copy-start | bytes 1572868
  27.0 15.2 %copy-start.1 = (bf16[1024,256]{1,0:T(8,128)(2,1)S(1)}, bf16[1024,256]{1,0:T(8,128)(2,1)}, u32[]{:S(2)}) copy-start(bf16[1024,256]{1,0:T(8,128)(2,1)} %cotangent.1) | copy-start | bytes 1572868

commit v9 on v6

--- a/solution.py
+++ b/solution.py
@@ -94,7 +94,7 @@
     left[...] = (dot(turned, tiles[...], 1, 0) * 0.5).astype(BF16) * m[...]
 
 
-def middle_kernel(plan, left, inner, cotangent, tiles, m, dmixed, part_left, activated, act, pres, dpres, sems):
+def middle_kernel(left, inner, cotangent, dmixed, part_left, activated, act, pres, dpres, sems):
     steps, copies = len(STEPS), []
     spans = [pl.ds(sum(STEPS[:s]), STEPS[s]) for s in range(steps)]
 
@@ -128,15 +128,15 @@
         copies.append(pltpu.make_async_copy(act.at[at, :], activated.at[at, :], sems.at[s]))
         copies[-1].start()
     total = products_of(steps - 1, total)
-    part = (total * 0.5).astype(BF16) * m[...]
-    part_left[...] = plan.turn(dot(part, tiles[...], 1, 1), GRADS_FIRST, True).astype(BF16)
+    part_left[...] = (total * 0.5).astype(BF16)
     for copy in copies:
         copy.wait()
 
 
-def last_kernel(plan, part, part_left, unspread, features, parts):
+def last_kernel(plan, part, part_left, unspread, features, tiles, m, parts):
+    left = plan.turn(dot(part_left[...] * m[...], tiles[...], 1, 1), GRADS_FIRST, True)
     part = dot(unspread[...], part[...], 1, 0).astype(BF16)
-    parts[...] = (dot(features[...], part, 1, 1) + part_left[...].astype(F32)).astype(BF16)
+    parts[...] = (dot(features[...], part, 1, 1) + left).astype(BF16)
 
 
 HBM = pl.BlockSpec(memory_space=pltpu.HBM)
@@ -189,9 +189,9 @@
     inner = exchange(inner.reshape(groups, -1, rows), "mp", MP_FIRST).reshape(width, rows)
 
     dmixed, part_left, activated = call(
-        functools.partial(middle_kernel, plan),
-        (left, inner, cotangent, tiles, m),
-        ((width, rows), tall, (rows, width)),
+        middle_kernel,
+        (left, inner, cotangent),
+        ((width, rows), square, (rows, width)),
         scratch=[
             pltpu.VMEM((rows, width), BF16),
             pltpu.VMEM((rows, width), F32),
@@ -205,7 +205,7 @@
     part = dot(dinner, tokens, 1, 0).astype(BF16) * block
     (parts,) = call(
         functools.partial(last_kernel, plan),
-        (part, part_left, unspread, gfeatures),
+        (part, part_left, unspread, gfeatures, tiles, m),
         (tall,),
     )
     sums = jnp.sum(exchange(parts.reshape(n_dp, *line), "dp", GRADS_FIRST).astype(F32), axis=0)

time: 75.6 us -> 75.6 us (level)
  no operation moved by 1% of the time
where the time goes in v9:
time: 75.6 us; the launch traced here: 75 us
  blocking collectives  70 us (93%)
  Pallas kernels  2.96 us (4%)
    all_to_all x4, blocking collectives, exchange(): lax.all_to_all(x, axis, 0, 0, axis_index_groups=[members], tiled=True)  70 us
    pallas_call x4, Pallas kernels, call(): pl.pallas_call(kernel, out_shape=outs, in_specs=[HBM if hbm_in else VMEM]...  2.96 us

profile of v9, /device:TPU:1, one launch (start us, length us, event | category | flops | bytes accessed | tf_op | source)
XLA Modules:
  0.0 75.0 jit_solution(6017298903634118543)
XLA Ops:
  0.6 0.0 copy-start
  0.6 0.9 %shard_map.67 = (bf16[32,4,2,128]{3,2,1,0:T(2,128)(2,1)S(1)}, bf16[256,128]{1,0:T(8,128)(2,1)S(1)}, bf16[128,256]{1,0:T(8,128)(2,1)S(1)}, bf16[128,256]{1,0:T(8,...) custom-call(bf16[4,2,64]{2,1,0:T(2,128)(2,1)} %right.1, ...), custom_call_target="tpu_custom_call" | custom-call | tf_op jit(solution)/shard_map/pallas_call | solution.py:151
  1.5 24.6 %all_to_all.20 = bf16[32,4,2,128]{3,2,1,0:T(2,128)(2,1)S(1)} all-to-all(bf16[32,4,2,128]{3,2,1,0:T(2,128)(2,1)S(1)} %get-tuple-element.16), channel_id=1, replica_groups={{416,432,448,464,480,496,0,16,32,48,64,80,96,112,128,144,160,176,192,20..., dimensions={0} | all-to-all | bytes 131072 | tf_op jit(solution)/shard_map/all_to_all | solution.py:22
  26.2 0.3 shard_map.68
  26.5 0.0 copy-done
  26.5 0.3 convolution_convert_fusion
  26.9 0.0 copy-start.1
  26.9 15.3 %all_to_all.21 = bf16[16,16,1024]{2,1,0:T(8,128)(2,1)S(1)} all-to-all(bf16[16,16,1024]{2,1,0:T(8,128)(2,1)S(1)} %bitcast.15), channel_id=1, replica_groups={{9,10,11,12,13,14,15,0,1,2,3,4,5,6,7,8},{25,26,27,28,29,30,31,16,17,18,..., dimensions={0} | all-to-all | bytes 1048576 | tf_op jit(solution)/shard_map/all_to_all | solution.py:22
  42.1 0.0 copy-done.1
  42.1 1.4 %shard_map.69 = (bf16[256,1024]{1,0:T(8,128)(2,1)S(1)}, bf16[256,256]{1,0:T(8,128)(2,1)S(1)}, bf16[1024,256]{1,0:T(8,128)(2,1)}) custom-call(bf16[256,256]{1,0:T(8,128)(2,1)S(1)} %get-tuple-element.22.left, bf16[256,1024]{1,0:T(8,128)(2,1)S(1)} %bitcast.10, bf16[1024,256]{1,0:T(8,128)(2,1)S(1)} %copy-done.1), custom_call_target="tpu_custom_call" | custom-call | tf_op jit(solution)/shard_map/pallas_call | solution.py:151
  43.5 12.6 %all_to_all.22 = bf16[16,16,1024]{2,1,0:T(8,128)(2,1)S(1)} all-to-all(bf16[16,16,1024]{2,1,0:T(8,128)(2,1)S(1)} %bitcast.11), channel_id=1, replica_groups={{9,10,11,12,13,14,15,0,1,2,3,4,5,6,7,8},{25,26,27,28,29,30,31,16,17,18,..., dimensions={0} | all-to-all | bytes 1048576 | tf_op jit(solution)/shard_map/all_to_all | solution.py:22
  56.1 0.3 fusion.part
  56.4 0.4 shard_map.70
  56.8 17.5 %all_to_all.23 = bf16[32,4,2,128]{3,2,1,0:T(2,128)(2,1)S(1)} all-to-all(bf16[32,4,2,128]{3,2,1,0:T(2,128)(2,1)S(1)} %bitcast.13), channel_id=1, replica_groups={{384,400,416,432,448,464,480,496,0,16,32,48,64,80,96,112,128,144,160,17..., dimensions={0} | all-to-all | bytes 131072 | tf_op jit(solution)/shard_map/all_to_all | solution.py:22
  74.3 0.1 convert_reduce_fusion
  74.4 0.7 fusion.1
Async XLA Ops:
  0.6 25.9 %copy-start = (bf16[1024,256]{1,0:T(8,128)(2,1)S(1)}, bf16[1024,256]{1,0:T(8,128)(2,1)}, u32[]{:S(2)}) copy-start(bf16[1024,256]{1,0:T(8,128)(2,1)} %param.4) | copy-start | bytes 1572868
  26.9 15.3 %copy-start.1 = (bf16[1024,256]{1,0:T(8,128)(2,1)S(1)}, bf16[1024,256]{1,0:T(8,128)(2,1)}, u32[]{:S(2)}) copy-start(bf16[1024,256]{1,0:T(8,128)(2,1)} %cotangent.1) | copy-start | bytes 1572868
